TPU v7x, 32 devices: a whole 2x2x4 slice. The times are simulated.
32 devices in a mesh: dp: 8 (over z, x), shard: 4 (over y, core).
Axes of the slice: x: 2, y: 2, z: 4, core: 2. Of those that a mesh axis runs over, the one named last changes fastest.
Arguments:
- tokens: bfloat16 [128, 3584], P('dp', 'shard'), may hold values from -6 to 6
- targets: bfloat16 [128, 3584], P('dp', 'shard'), may hold values from -6 to 6
- task_of_token: int32 [128], P('dp'), may hold values from 0 to 15, never falling along the last dimension, each value on 1 to 16 neighbouring positions
- up_weight: bfloat16 [18944, 3584], P('dp', 'shard'), may hold values from -0.09375 to 0.09375
- down_weight: bfloat16 [18944, 3584], P('dp', 'shard'), may hold values from -0.046875 to 0.046875
- outer_up: bfloat16 [18944, 3584], P('dp', 'shard'), may hold values from -6 to 6
- outer_down: bfloat16 [18944, 3584], P('dp', 'shard'), may hold values from -6 to 6
Outputs:
- meta_up: float32 [18944, 3584], P('dp', 'shard')
- meta_down: float32 [18944, 3584], P('dp', 'shard')
Inputs may be any that keep to these rules, and one draw needn't show every extreme that they name: `task_of_token`: task numbers never fall along the tokens; every task has 1 to 16 tokens, and some task has exactly 16.
All inputs are finite; a program needn't handle non-finite values.
Results may differ from a plain program's by a relative error of at most 0.001.
Values may be sent and summed in bfloat16 or wider, within the bound.
A program may use at most 64 MiB of HBM per device.

v0:
```python
import functools

import jax
import jax.numpy as jnp
from jax import lax
from jax.experimental import pallas as pl
from jax.experimental.pallas import tpu as pltpu
from jax.sharding import PartitionSpec as P

TASKS = 16
BF = jnp.bfloat16
F32 = jnp.float32
MESH = pl.DeviceIdType.MESH
VM = pl.BlockSpec(memory_space=pltpu.VMEM)


def sigmoid_parts(linear_part):
    argument = linear_part.astype(F32)
    logistic = jax.nn.sigmoid(argument)
    derivative = logistic * (1.0 + argument * (1.0 - logistic))
    second_order = logistic * (1.0 - logistic) * (2.0 + argument * (1.0 - 2.0 * logistic))
    return (argument * logistic, derivative, second_order)


def contract_last(left_side, right_side):
    return lax.dot_general(
        left_side, right_side, (((1,), (1,)), ((), ())), preferred_element_type=F32
    )


def contract_first(left_side, right_side):
    return lax.dot_general(
        left_side, right_side, (((0,), (0,)), ((), ())), preferred_element_type=F32
    )


def product(left_side, right_side):
    return jnp.dot(left_side, right_side, preferred_element_type=F32)


def remote(src, dst, send_sem, recv_sem, where):
    return pltpu.make_async_remote_copy(
        src_ref=src,
        dst_ref=dst,
        send_sem=send_sem,
        recv_sem=recv_sem,
        device_id=where,
        device_id_type=MESH,
    )


def greet(places):
    barrier = pltpu.get_barrier_semaphore()
    for place in places:
        pl.semaphore_signal(barrier, inc=1, device_id=place, device_id_type=MESH)
    pl.semaphore_wait(barrier, len(places))


def rows_at(index, count):
    return pl.ds(pl.multiple_of(index * count, count), count)


def call(kernel, outs, scratch, number, args, far=0):
    return pl.pallas_call(
        kernel,
        out_shape=outs,
        in_specs=[pl.BlockSpec(memory_space=pl.ANY)] * far + [VM] * (len(args) - far),
        out_specs=[VM] * len(outs),
        scratch_shapes=scratch,
        compiler_params=pltpu.CompilerParams(
            collective_id=number, has_side_effects=True, vmem_limit_bytes=48 * 2**20
        ),
    )(*args)


def ring_places(axis, n):
    me = lax.axis_index(axis)
    return me, [{axis: lax.rem(me + k, n)} for k in range(1, n)], [
        lax.rem(me + k, n) for k in range(1, n)
    ]


def gather_kernel(
    n, count, up_ref, down_ref, *refs
):
    ins, outs, norm_ref = refs[:count], refs[count : 2 * count], refs[2 * count]
    held, load_sem, send_sem, recv_sem = refs[2 * count + 1 :]
    loads = [
        pltpu.make_async_copy(src, held.at[i], load_sem.at[i])
        for i, src in enumerate((up_ref, down_ref))
    ]
    for load in loads:
        load.start()
    me, places, _ = ring_places("dp", n)
    for src, dst in zip(ins, outs):
        dst[rows_at(me, src.shape[0]), :] = src[...]
    greet(places)
    copies = []
    for k, place in enumerate(places):
        for i, (src, dst) in enumerate(zip(ins, outs)):
            rows = rows_at(me, src.shape[0])
            copies.append(
                remote(src, dst.at[rows, :], send_sem.at[i, k], recv_sem.at[i, k], place)
            )
            copies[-1].start()
    size, width = up_ref.shape
    total = jnp.zeros((16, width), F32)
    for i, load in enumerate(loads):
        load.wait()

        def add(step, value, i=i):
            block = held[i, rows_at(step, 16), :].astype(F32)
            return value + block * block

        total = lax.fori_loop(0, size // 16, add, total)
    number = jnp.sum(jnp.sum(total, axis=1, keepdims=True), axis=0, keepdims=True)
    norm_ref[...] = jnp.broadcast_to(number, norm_ref.shape)
    for copy in copies:
        copy.wait()


def gather_dp(n, number, up, down, *arrays):
    count = len(arrays)
    outs = [jax.ShapeDtypeStruct((n * a.shape[0], a.shape[1]), a.dtype) for a in arrays]
    outs.append(jax.ShapeDtypeStruct((8, 128), F32))
    scratch = [pltpu.VMEM((2,) + up.shape, up.dtype), pltpu.SemaphoreType.DMA((2,))]
    scratch += [pltpu.SemaphoreType.DMA((count, n - 1))] * 2
    return call(
        functools.partial(gather_kernel, n, count), outs, scratch, number, (up, down) + arrays, 2
    )


def sum_kernel(n, count, bits, *refs):
    ins, outs = refs[:count], refs[count : 2 * count]
    halves, accs, wires = (refs[(2 + j) * count : (3 + j) * count] for j in range(3))
    send_sem, recv_sem = refs[5 * count :]
    me = lax.axis_index("shard")

    def flip(bit):
        step = 1 << bit
        return {"shard": me + step - 2 * step * lax.rem(me // step, 2)}

    greet([flip(bit) for bit in range(bits)])
    low = lax.rem(me, 2)
    first = []
    for i in range(count):
        half = ins[i].shape[0] // 2
        first.append(
            remote(
                ins[i].at[rows_at(1 - low, half), :],
                halves[i],
                send_sem.at[i, 0],
                recv_sem.at[i, 0],
                flip(0),
            )
        )
        first[-1].start()
    now = []
    for i in range(count):
        half = ins[i].shape[0] // 2
        first[i].wait()
        total = ins[i][rows_at(low, half), :].astype(F32) + halves[i][...].astype(F32)
        accs[i][0] = total.astype(ins[i].dtype)
        if bits > 1:
            copy = remote(
                accs[i].at[0], wires[i].at[0], send_sem.at[i, 1], recv_sem.at[i, 1], flip(1)
            )
            copy.start()
            now.append(copy)
    last = []
    for i in range(count):
        half = ins[i].shape[0] // 2
        mine = rows_at(low, half)
        for bit in range(1, bits):
            now[i].wait()
            total = accs[i][bit - 1].astype(F32) + wires[i][bit - 1].astype(F32)
            accs[i][bit] = total.astype(ins[i].dtype)
            if bit + 1 < bits:
                now[i] = remote(
                    accs[i].at[bit],
                    wires[i].at[bit],
                    send_sem.at[i, bit + 1],
                    recv_sem.at[i, bit + 1],
                    flip(bit + 1),
                )
                now[i].start()
        outs[i][mine, :] = accs[i][bits - 1]
        copy = remote(
            accs[i].at[bits - 1],
            outs[i].at[mine, :],
            send_sem.at[i, bits],
            recv_sem.at[i, bits],
            flip(0),
        )
        copy.start()
        last.append(copy)
    for copy in last:
        copy.wait()


def sum_shard(n, number, *arrays):
    count = len(arrays)
    bits = n.bit_length() - 1
    outs = [jax.ShapeDtypeStruct(a.shape, a.dtype) for a in arrays]
    sizes = [(a.shape[0] // 2, a.shape[1]) for a in arrays]
    scratch = [pltpu.VMEM(s, a.dtype) for s, a in zip(sizes, arrays)]
    scratch += [pltpu.VMEM((bits,) + s, a.dtype) for s, a in zip(sizes, arrays)]
    scratch += [pltpu.VMEM((max(bits - 1, 1),) + s, a.dtype) for s, a in zip(sizes, arrays)]
    scratch += [pltpu.SemaphoreType.DMA((count, bits + 1))] * 2
    return call(functools.partial(sum_kernel, n, count, bits), outs, scratch, number, arrays)


def error_kernel(
    n, y_ref, z_ref, targets_ref, weight_ref, e_ref, t_ref, row_ref,
    held, fresh, send_sem, recv_sem, send_two, recv_two,
):
    rows = targets_ref.shape[0]
    me, places, peers = ring_places("dp", n)
    greet(places)
    copies = []
    for i, part in enumerate((y_ref, z_ref)):
        for k in range(n - 1):
            copy = remote(
                part.at[rows_at(peers[k], rows), :],
                held.at[i, k],
                send_sem.at[i, k],
                recv_sem.at[i, k],
                places[k],
            )
            copy.start()
            copies.append(copy)
    mine = rows_at(me, rows)
    weight = weight_ref[:, 0:1]
    second = []
    for i, part in enumerate((y_ref, z_ref)):
        total = part[mine, :].astype(F32)
        for k in range(n - 1):
            copies[i * (n - 1) + k].wait()
            total = total + held[i, k].astype(F32)
        if i == 0:
            value = (weight * (total - targets_ref[...].astype(F32))).astype(BF)
        else:
            row_ref[...] = total
            value = (weight * total).astype(BF)
        dst = (e_ref, t_ref)[i]
        fresh[i] = value
        dst[mine, :] = value
        for k in range(n - 1):
            copy = remote(
                fresh.at[i], dst.at[mine, :], send_two.at[i, k], recv_two.at[i, k], places[k]
            )
            copy.start()
            second.append(copy)
    for copy in second:
        copy.wait()


def all_errors(n, number, y, z, targets, weight):
    rows, width = targets.shape
    outs = [jax.ShapeDtypeStruct(y.shape, BF)] * 2 + [jax.ShapeDtypeStruct((rows, width), F32)]
    scratch = [pltpu.VMEM((2, n - 1, rows, width), BF), pltpu.VMEM((2, rows, width), BF)]
    scratch += [pltpu.SemaphoreType.DMA((2, n - 1))] * 4
    return call(
        functools.partial(error_kernel, n), outs, scratch, number, (y, z, targets, weight)
    )


def totals_kernel(
    n, m, w_ref, row_ref, weight_ref, part_ref, norm_ref, hidden_ref, tangent_ref, gate_ref,
    token_ref, error_ref, out_ref,
    held, dp_slots, shard_slots, own, send_sem, recv_sem, send_two, recv_two, send_three, recv_three,
):
    rows = row_ref.shape[0]
    me, places, peers = ring_places("dp", n)
    own_shard, shard_places, _ = ring_places("shard", m)
    greet(places + shard_places)
    copies = []
    for k in range(n - 1):
        copy = remote(
            w_ref.at[rows_at(peers[k], rows), :],
            held.at[k],
            send_sem.at[k],
            recv_sem.at[k],
            places[k],
        )
        copy.start()
        copies.append(copy)
    count = gate_ref.shape[0]

    def summed(term):
        return jnp.sum(jnp.sum(term, axis=1, keepdims=True), axis=0, keepdims=True)

    head, tail = pl.ds(0, count), pl.ds(count, count)
    errors, crossed = error_ref[head, head], error_ref[tail, head]
    tangents = tangent_ref[...]
    s_e = summed(tangents * errors)
    h_t = summed(hidden_ref[head, head] * crossed)
    change = summed(gate_ref[...] * token_ref[...]) + s_e + 2.0 * h_t
    change = change + summed(hidden_ref[head, tail] * error_ref[tail, tail])
    carry = summed(hidden_ref[tail, head] * errors)
    carry = carry + summed(hidden_ref[tail, tail] * error_ref[head, tail])
    total = w_ref[rows_at(me, rows), :].astype(F32)
    for k in range(n - 1):
        copies[k].wait()
        total = total + held[k].astype(F32)
    row, weight = row_ref[...], weight_ref[:, 0:1]
    index = lax.broadcasted_iota(jnp.int32, part_ref.shape, 0)
    value = part_ref[...]
    for place, number in ((2, change), (3, s_e + h_t), (4, 2.0 * carry)):
        value = value + jnp.where(index == place, number, 0.0)
    value = value + jnp.where(index == 0, norm_ref[...], 0.0)
    for place, term in ((1, row * row), (3, row * total), (4, total * total)):
        number = summed(weight * term)
        value = value + jnp.where(index == place, number, 0.0)
    own[0] = value
    dp_slots[pl.ds(me, 1)] = value[None]
    copies = []
    for k in range(n - 1):
        copy = remote(
            own.at[0], dp_slots.at[me], send_two.at[k], recv_two.at[k], places[k]
        )
        copy.start()
        copies.append(copy)
    for copy in copies:
        copy.wait()
    value = dp_slots[0]
    for k in range(1, n):
        value = value + dp_slots[k]
    own[1] = value
    shard_slots[pl.ds(own_shard, 1)] = value[None]
    copies = []
    for k in range(m - 1):
        copy = remote(
            own.at[1],
            shard_slots.at[own_shard],
            send_three.at[k],
            recv_three.at[k],
            shard_places[k],
        )
        copy.start()
        copies.append(copy)
    for copy in copies:
        copy.wait()
    value = shard_slots[0]
    for k in range(1, m):
        value = value + shard_slots[k]
    own[2] = value
    norm, first, change, mixed, final = (own[2, i : i + 1, :] for i in range(5))
    step = norm / (norm + first)
    keep = first / (norm + first)
    norm_next = keep * keep * norm - 2.0 * keep * step * first + step * step * change
    ratio = norm_next / norm
    curvature = (
        norm_next
        + keep * keep * first
        - 2.0 * keep * step * mixed
        + step * step * final
        - ratio * norm_next / step
    )
    step_next = norm_next / curvature
    out_ref[0:1, :] = step + step_next * (ratio + keep)
    out_ref[1:2, :] = -step_next * step


def all_totals(n, m, number, w, row, weight, part, *others):
    scratch = [
        pltpu.VMEM((n - 1,) + row.shape, BF),
        pltpu.VMEM((n,) + part.shape, F32),
        pltpu.VMEM((m,) + part.shape, F32),
        pltpu.VMEM((3,) + part.shape, F32),
    ]
    scratch += [pltpu.SemaphoreType.DMA((n - 1,))] * 4 + [pltpu.SemaphoreType.DMA((m - 1,))] * 2
    outs = [jax.ShapeDtypeStruct((2, 128), F32)]
    return call(
        functools.partial(totals_kernel, n, m), outs, scratch, number, (w, row, weight, part) + others
    )[0]


def two_halves(matrix):
    high = matrix.astype(BF)
    return high, (matrix - high.astype(F32)).astype(BF)


def body(n, m, tokens, targets, task_of_token, up_weight, down_weight, outer_up, outer_down):
    rows = tokens.shape[0]
    count = rows * n
    task_block = jnp.broadcast_to(task_of_token.astype(F32)[:, None], (rows, 128))
    gathered, all_tasks, start_norm = gather_dp(n, 0, outer_up, outer_down, tokens, task_block)
    same = (task_block[:, 0:1] == all_tasks[:, 0][None, :]).astype(F32)
    weight = 1.0 / (TASKS * jnp.sum(same, axis=1, keepdims=True))
    weight = jnp.broadcast_to(weight, (rows, 128))

    linear_part, tangent_linear = sum_shard(
        m,
        1,
        contract_last(gathered, up_weight).astype(BF),
        contract_last(gathered, outer_up).astype(BF),
    )
    activation, derivative, second_order = sigmoid_parts(linear_part)
    hidden = activation.astype(BF)
    tangent = tangent_linear.astype(F32)
    tangent_hidden = (derivative * tangent).astype(BF)

    both = product(jnp.concatenate([hidden, tangent_hidden], axis=0), down_weight)
    errors, tangent_errors, tangent_row = all_errors(
        n,
        2,
        both[:count].astype(BF),
        (both[count:] + product(hidden, outer_down)).astype(BF),
        targets,
        weight,
    )

    two_errors = jnp.concatenate([errors, tangent_errors], axis=0)
    back = contract_last(two_errors, down_weight)
    backward = back[:count]
    through_outer = contract_last(errors, outer_down)
    curved = second_order * backward
    gate_part = derivative * (back[count:] + through_outer) + curved * tangent
    token_gram = contract_last(gathered, gathered)
    tangent_gate, full_gram = sum_shard(m, 3, gate_part.astype(BF), token_gram)

    high, low = two_halves(full_gram)
    lowered = product(
        jnp.concatenate([high, low], axis=1),
        jnp.concatenate([tangent_gate, tangent_gate], axis=0),
    )
    carried = (derivative * lowered).astype(BF)
    hidden_gram = contract_last(
        jnp.concatenate([hidden, carried], axis=0),
        jnp.concatenate([tangent_hidden, hidden], axis=0),
    )
    tangent_gram = contract_last(tangent_hidden, tangent_hidden)
    error_gram = contract_last(two_errors, two_errors)
    further = product(carried, down_weight) + product(
        hidden_gram[:count].astype(BF), two_errors
    )

    crossing = through_outer
    first_term = jnp.sum(
        2.0 * tangent_hidden.astype(F32) * crossing + curved * tangent * tangent
    )
    mixed_term = jnp.sum(carried.astype(F32) * crossing + curved * tangent * lowered)
    last_term = jnp.sum(curved * lowered * lowered)
    gate_gram = contract_last(tangent_gate, tangent_gate)
    index = lax.broadcasted_iota(jnp.int32, (8, 128), 0)
    part = jnp.zeros((8, 128), F32)
    for place, value in ((1, first_term), (3, mixed_term), (4, last_term)):
        part = part + jnp.where(index == place, value, 0.0)

    sums = all_totals(
        n,
        m,
        4,
        further.astype(BF),
        tangent_row,
        weight,
        part,
        start_norm,
        hidden_gram,
        tangent_gram,
        gate_gram,
        token_gram,
        error_gram,
    )
    of_outer, of_change = sums[0, 0], sums[1, 0]
    change_up = contract_first(tangent_gate, gathered)
    change_down = contract_first(
        jnp.concatenate([tangent_hidden, hidden], axis=0), two_errors
    )
    return (
        of_outer * outer_up.astype(F32) + of_change * change_up,
        of_outer * outer_down.astype(F32) + of_change * change_down,
    )


def solution(mesh):
    placed = tuple(P("dp") if i == 2 else P("dp", "shard") for i in range(7))
    return jax.shard_map(
        functools.partial(body, mesh.shape["dp"], mesh.shape["shard"]),
        mesh=mesh,
        in_specs=placed,
        out_specs=(P("dp", "shard"), P("dp", "shard")),
        check_vma=False,
    )
```

profile of v0, /device:TPU:0, one launch (start us, length us, event | category | flops | bytes accessed | tf_op | source)
XLA Modules:
  0.0 131.5 jit_solution(10728690006687859911)
XLA Ops:
  0.6 0.7 convert_element_type.59
  1.3 0.1 broadcast_in_dim.28.refs_1_
  1.4 0.0 copy-start
  1.4 2.2 %copy-done = bf16[2368,896]{1,0:T(8,128)(2,1)S(1)} copy-done((bf16[2368,896]{1,0:T(8,128)(2,1)S(1)}, bf16[2368,896]{1,0:T(8,128)(2,1)}, u32[]{:S(2)}) %copy-start) | copy-done | bytes 4243480
  3.6 0.0 copy-start.2
  3.6 0.7 copy-done.2
  4.3 11.7 %shard_map.86 = (bf16[128,896]{1,0:T(8,128)(2,1)S(1)}, f32[128,128]{1,0:T(8,128)S(1)}, f32[8,128]{1,0:T(8,128)S(1)}) custom-call(bf16[2368,896]{1,0:T(8,128)(2,1)S(1)} %copy-done, bf16[2368,896]{1,0:T(8,128)(2,1)} %down_ref.1, bf16[16,896]{1,0:T(8,128)(2,1)S(1)} %copy-done.2, f32[16,128]{1,0:T(8,128)S(1)} %broadcast_in_dim.28.refs_1_), custom_call_target="tpu_custom_call" | custom-call | tf_op jit(solution)/shard_map/pallas_call | solution.py:64
  16.0 0.1 slice_reduce_fusion
  16.2 0.2 convert_reduce_fusion
  16.3 0.1 broadcast_in_dim.29.weight_ref
  16.4 0.2 fusion.39.refs_1_.token_ref
  16.7 1.3 convolution_convert_fusion
  18.0 0.3 copy.32.refs_1_
  18.3 3.5 %convolution_convert_fusion.1 = bf16[128,2368]{0,1:T(8,128)(2,1)S(1)} fusion(bf16[128,896]{1,0:T(8,128)(2,1)S(1)} %get-tuple-element.12, bf16[2368,896]{1,0:T(8,128)(2,1)} %param.10), kind=kOutput, calls=%fused_computation.3 | convolution fusion | flops 543465472 | bytes 5079040 | tf_op jit(solution)/shard_map/dot_general | solution.py:26
  21.7 0.3 copy.31.refs_0_
  22.1 19.4 %shard_map.87 = (bf16[128,2368]{1,0:T(8,128)(2,1)S(1)}, bf16[128,2368]{1,0:T(8,128)(2,1)S(1)}) custom-call(bf16[128,2368]{1,0:T(8,128)(2,1)S(1)} %copy.31.refs_0_, bf16[128,2368]{1,0:T(8,128)(2,1)S(1)} %copy.32.refs_1_), custom_call_target="tpu_custom_call" | custom-call | tf_op jit(solution)/shard_map/pallas_call | solution.py:64
  41.5 0.6 fusion.4
  42.1 0.0 slice-start.2
  42.1 0.3 fusion.40.tangent_ref
  42.5 0.0 slice-start.3
  42.5 0.0 slice-start.4
  42.5 3.9 %fusion = f32[256,896]{1,0:T(8,128)S(1)} fusion(bf16[2368,896]{1,0:T(8,128)(2,1)} %param.11, bf16[128,2368]{1,0:T(8,128)(2,1)S(1)} %get-tuple-element.29, bf16[128,2368]{1,0:T(8,128)(2,1)S(1)} %get-tuple-element.28), kind=kOutput, calls=%fused_computation.15 | convolution fusion | flops 1088749568 | bytes 6373376 | tf_op jit(solution)/shard_map/dot_general | solution.py:38
  46.4 0.0 slice-done.2
  46.4 0.0 slice-done.3
  46.4 0.0 copy-start.1
  46.5 0.0 slice-start.5
  46.5 1.0 fusion.24.z_ref
  47.5 0.0 copy-done.1
  47.5 26.7 %shard_map.88 = (bf16[128,896]{1,0:T(8,128)(2,1)S(1)}, bf16[128,896]{1,0:T(8,128)(2,1)S(1)}, f32[16,896]{1,0:T(8,128)S(1)}) custom-call(bf16[128,896]{1,0:T(8,128)(2,1)S(1)} %slice.61.y_ref, bf16[128,896]{1,0:T(8,128)(2,1)S(1)} %fusion.24.z_ref, bf16[16,896]{1,0:T(8,128)(2,1)S(1)} %copy-done.1, f32[16,128]{1,0:T(8,128)S(1)} %broadcast_in_dim.29.weight_ref), custom_call_target="tpu_custom_call" | custom-call | tf_op jit(solution)/shard_map/pallas_call | solution.py:64
  74.3 0.3 fusion.42.error_ref
  74.6 0.0 slice-done.4
  74.6 0.0 slice-done.5
  74.7 1.6 %fusion.38 = f32[256,2368]{1,0:T(8,128)S(1)} fusion(bf16[256,896]{1,0:T(8,128)(2,1)S(1)} %constant_dynamic-update-slice_fusion, bf16[2368,896]{1,0:T(8,128)(2,1)S(1)} %bitcast.31), kind=kOutput, calls=%fused_computation.69 | convolution fusion | flops 1086324736 | bytes 7127040 | tf_op jit(solution)/shard_map/dot_general | solution.py:26
  76.2 1.5 %fusion.17 = (bf16[128,2368]{1,0:T(8,128)(2,1)S(1)}, f32[128,2368]{1,0:T(8,128)S(1)}) fusion(f32[256,2368]{1,0:T(8,128)S(1)} %fusion.38, bf16[128,2368]{1,0:T(8,128)(2,1)S(1)} %get-tuple-element.14, bf16[128,2368]{1,0:T(8,128)(2,1)S(1)} %get-tuple-element.13, bf16[128,896]{1,0:T(8,128)(2,1)S(1)} %get-tuple-element.16, bf16[2368,896]{1,0:T(8,128)(2,1)S(1)} %bitcast.29), kind=kOutput, calls=%fused_computation.33 | convolution fusion | flops 549527552 | bytes 9928704 | tf_op jit(solution)/shard_map/dot_general | solution.py:26
  77.8 13.1 %shard_map.89 = (bf16[128,2368]{1,0:T(8,128)(2,1)S(1)}, f32[128,128]{1,0:T(8,128)S(1)}) custom-call(bf16[128,2368]{1,0:T(8,128)(2,1)S(1)} %get-tuple-element.32.refs_0_, f32[128,128]{1,0:T(8,128)S(1)} %fusion.39.refs_1_.token_ref), custom_call_target="tpu_custom_call" | custom-call | tf_op jit(solution)/shard_map/pallas_call | solution.py:64
  90.9 2.2 %fusion.6 = (f32[]{:T(128)}, f32[]{:T(128)}, f32[]{:T(128)}, bf16[128,2368]{1,0:T(8,128)(2,1)S(1)}) fusion(bf16[128,2368]{1,0:T(8,128)(2,1)S(1)} %get-tuple-element.14, f32[128,2368]{1,0:T(8,128)S(1)} %get-tuple-element.33, bf16[128,2368]{1,0:T(8,128)(2,1)S(1)} %get-tuple-element.28, f32[256,2368]{1,0:T(8,128)S(1)} %fusion.38, ...), kind=kOutput, calls=%fused_computation.21 | convolution fusion | flops 167747584 | bytes 5521420 | tf_op jit(solution)/shard_map/dot_general | solution.py:38
  93.1 1.9 %fusion.31 = f32[8]{0:T(128)S(1)} fusion(f32[]{:T(128)} %get-tuple-element.24, f32[]{:T(128)} %get-tuple-element.23, f32[]{:T(128)} %get-tuple-element.22), kind=kLoop, calls=%fused_computation.62 | loop fusion | flops 64 | bytes 44 | tf_op jit(solution)/shard_map/add | solution.py:449
  95.0 0.1 iota.13.part_ref
  95.1 0.3 fusion.41.gate_ref
  95.4 0.7 fusion.1.hidden_ref
  96.2 0.2 fusion.26
  96.4 0.0 slice-start
  96.4 3.1 %fusion.25.w_ref = bf16[128,896]{1,0:T(8,128)(2,1)S(1)} fusion(f32[128,896]{1,0:T(8,128)S(1)} %fusion.26, bf16[128,2368]{1,0:T(8,128)(2,1)S(1)} %get-tuple-element.25, bf16[2368,896]{1,0:T(8,128)(2,1)} %param.11), kind=kOutput, calls=%fused_computation.46 | convolution fusion | flops 543391744 | bytes 5537792 | tf_op jit(solution)/shard_map/dot_general | solution.py:38
  99.5 18.8 %shard_map.90 = f32[2,128]{1,0:T(2,128)S(1)} custom-call(bf16[128,896]{1,0:T(8,128)(2,1)S(1)} %fusion.25.w_ref, f32[16,896]{1,0:T(8,128)S(1)} %get-tuple-element.20.row_ref, f32[16,128]{1,0:T(8,128)S(1)} %broadcast_in_dim.29.weight_ref, f32[8,128]{1,0:T(8,128)S(1)} %iota.13.part_ref, f32[8,128]{1,0:T(8,128)S(1)} %get-tuple-element.21.norm_ref, ...), custom_call_target="tpu_custom_call" | custom-call | tf_op jit(solution)/shard_map/pallas_call | solution.py:64
  118.3 0.6 fusion.37
  118.9 0.0 slice-start.1
  118.9 6.6 %multiply_add_fusion = f32[2368,896]{1,0:T(8,128)} fusion(bf16[2368,896]{1,0:T(8,128)(2,1)S(1)} %bitcast.29, bf16[256,896]{1,0:T(8,128)(2,1)S(1)} %constant_dynamic-update-slice_fusion, f32[]{:T(128)} %bitcast.1, f32[]{:T(128)} %bitcast, bf16[128,2368]{1,0:T(8,128)(2,1)S(1)} %get-tuple-element.29, bf16[128,2368]{1,0:T(8,128)(2,1)S(1)} %get-tuple-element.28), kind=kOutput, calls=%fused_computation | convolution fusion | flops 1097236480 | bytes 14401544 | tf_op jit(solution)/shard_map/dot_general | solution.py:32
  125.5 0.0 slice-done
  125.5 0.0 slice-done.1
  125.5 6.0 %multiply_add_fusion.1 = f32[2368,896]{1,0:T(8,128)} fusion(bf16[2368,896]{1,0:T(8,128)(2,1)S(1)} %bitcast.27, bf16[128,2368]{1,0:T(8,128)(2,1)S(1)} %get-tuple-element.19, bf16[128,896]{1,0:T(8,128)(2,1)S(1)} %get-tuple-element.12, f32[]{:T(128)} %bitcast.1, f32[]{:T(128)} %bitcast), kind=kOutput, calls=%fused_computation.1 | convolution fusion | flops 551649280 | bytes 13565960 | tf_op jit(solution)/shard_map/dot_general | solution.py:32
  (8 shorter events, 0.1 us)
Async XLA Ops:
  1.4 2.2 %copy-start = (bf16[2368,896]{1,0:T(8,128)(2,1)S(1)}, bf16[2368,896]{1,0:T(8,128)(2,1)}, u32[]{:S(2)}) copy-start(bf16[2368,896]{1,0:T(8,128)(2,1)} %up_ref.1) | copy-start | bytes 12730372
  3.6 0.7 copy-start.2
  42.1 4.3 %slice-start.2 = ((s8[4243456]{0:T(1024)(128)(4,1)}), s8[4194304]{0:T(1024)(128)(4,1)S(1)}, s32[]{:S(2)}) async-start(s8[4243456]{0:T(1024)(128)(4,1)} %bitcast.28), calls=%async_computation.2 | async-start | bytes 8388608
  42.5 3.9 %slice-start.3 = ((s8[4243456]{0:T(1024)(128)(4,1)}), s8[49152]{0:T(1024)(128)(4,1)S(1)}, s32[]{:S(2)}) async-start(s8[4243456]{0:T(1024)(128)(4,1)} %bitcast.28), calls=%async_computation.3 | async-start | bytes 98304
  42.5 32.1 %slice-start.4 = ((s8[4243456]{0:T(1024)(128)(4,1)}), s8[4194304]{0:T(1024)(128)(4,1)S(1)}, s32[]{:S(2)}) async-start(s8[4243456]{0:T(1024)(128)(4,1)} %bitcast.30), calls=%async_computation.4 | async-start | bytes 8388608
  46.4 1.0 copy-start.1
  46.5 28.2 %slice-start.5 = ((s8[4243456]{0:T(1024)(128)(4,1)}), s8[49152]{0:T(1024)(128)(4,1)S(1)}, s32[]{:S(2)}) async-start(s8[4243456]{0:T(1024)(128)(4,1)} %bitcast.30), calls=%async_computation.5 | async-start | bytes 98304
  96.4 29.0 %slice-start = ((s8[4243456]{0:T(1024)(128)(4,1)}), s8[49152]{0:T(1024)(128)(4,1)S(1)}, s32[]{:S(2)}) async-start(s8[4243456]{0:T(1024)(128)(4,1)} %bitcast.26), calls=%async_computation | async-start | bytes 98304
  118.9 6.6 %slice-start.1 = ((s8[4243456]{0:T(1024)(128)(4,1)}), s8[4194304]{0:T(1024)(128)(4,1)S(1)}, s32[]{:S(2)}) async-start(s8[4243456]{0:T(1024)(128)(4,1)} %bitcast.26), calls=%async_computation.1 | async-start | bytes 8388608
where the time goes:
time: 132 us; the launch traced here: 131 us
  Pallas kernels  89.8 us (68%)
  matrix products  32.8 us (25%)
  local copies, waits for them, and re-layouts  4.57 us (3%)
  other arithmetic  3.38 us (3%)
    pallas_call x5, Pallas kernels, call(): pl.pallas_call(kernel, out_shape=outs, in_specs=[pl.BlockSpec(memory_spac...  89.8 us
    dot_general x2, matrix products, contract_first(): lax.dot_general(left_side, right_side, (((0,), (0,)), ((), ())), preferre...  12.6 us
    dot_general x5, matrix products, product(): return jnp.dot(left_side, right_side, preferred_element_type=F32)  10.3 us
    dot_general x9, matrix products, contract_last(): lax.dot_general(left_side, right_side, (((1,), (1,)), ((), ())), preferre...  9.83 us
    unnamed x19, local copies, waits for them, and re-layouts  3.02 us

commit v1 on v0

v1 whole, which is shorter than its diff:
```python
import functools
import types

import jax
import jax.numpy as jnp
from jax import lax
from jax.experimental import pallas as pl
from jax.experimental.pallas import tpu as pltpu
from jax.sharding import PartitionSpec as P

TASKS = 16
STEPS = 4
BF = jnp.bfloat16
F32 = jnp.float32
MESH = pl.DeviceIdType.MESH
VMEM_LIMIT = 60 * 2**20


def sigmoid_parts(linear_part):
    argument = linear_part.astype(F32)
    logistic = jax.nn.sigmoid(argument)
    derivative = logistic * (1.0 + argument * (1.0 - logistic))
    second_order = logistic * (1.0 - logistic) * (2.0 + argument * (1.0 - 2.0 * logistic))
    return (argument * logistic, derivative, second_order)


def contract_last(left_side, right_side):
    return lax.dot_general(
        left_side, right_side, (((1,), (1,)), ((), ())), preferred_element_type=F32
    )


def contract_first(left_side, right_side):
    return lax.dot_general(
        left_side, right_side, (((0,), (0,)), ((), ())), preferred_element_type=F32
    )


def product(left_side, right_side):
    return jnp.dot(left_side, right_side, preferred_element_type=F32)


def remote(src, dst, send_sem, recv_sem, where):
    return pltpu.make_async_remote_copy(
        src_ref=src,
        dst_ref=dst,
        send_sem=send_sem,
        recv_sem=recv_sem,
        device_id=where,
        device_id_type=MESH,
    )


def summed(term):
    return jnp.sum(jnp.sum(term, axis=1, keepdims=True), axis=0, keepdims=True)


def folded(term):
    return jnp.sum(term.reshape(term.shape[0] // 8, 8, term.shape[1]), axis=0)


def span(start, size, unit):
    return pl.ds(pl.multiple_of(start, unit), size)


def fused_kernel(n, m, hid, names, *refs):
    r = types.SimpleNamespace(**dict(zip(names, refs)))
    rows, width = r.tokens.shape
    count, half, nz = n * rows, n * rows // 2, n // 2
    total = r.w.shape[1]
    hp = total // 2
    h = hp // STEPS
    bits = m.bit_length() - 1
    me = lax.axis_index("dp")
    xx, zz = lax.rem(me, 2), me // 2
    shard = lax.axis_index("shard")
    low = lax.rem(shard, 2)
    mine, other = low * hp, (1 - low) * hp
    partner = {"dp": 2 * zz + 1 - xx}
    column = [{"dp": 2 * lax.rem(zz + k, nz) + xx} for k in range(1, nz)]
    dp_places = [{"dp": lax.rem(me + k, n)} for k in range(1, n)]
    shard_places = [{"shard": lax.rem(shard + k, m)} for k in range(1, m)]

    def flip(bit):
        step = 1 << bit
        return {"shard": shard + step - 2 * step * lax.rem(shard // step, 2)}

    loads = [
        pltpu.make_async_copy(src, r.w.at[i, pl.ds(0, hid)], r.load_sem.at[i])
        for i, src in enumerate((r.up, r.outer_up, r.down, r.outer_down))
    ]
    for load in loads:
        load.start()

    lane = lax.broadcasted_iota(jnp.int32, (8, 128), 1)
    line = lax.broadcasted_iota(jnp.int32, (rows, 128), 0)
    own_row = jnp.full((8, 128), -1.0, F32)
    own_col = jnp.zeros((rows, 128), F32)
    for i in range(rows):
        number = r.task[i].astype(F32)
        own_row = jnp.where(lane == i, number, own_row)
        own_col = jnp.where(line == i, number, own_col)
    r.task_own[...] = own_row
    place = xx * nz + zz
    block = span(place * rows, rows, rows)
    r.xx[block, :] = r.tokens[...]
    if total > hid:
        r.w[:, pl.ds(hid, total - hid), :] = jnp.zeros((4, total - hid, width), BF)
    r.acc[...] = jnp.zeros(r.acc.shape, F32)

    barrier = pltpu.get_barrier_semaphore()
    for where in dp_places + shard_places:
        pl.semaphore_signal(barrier, inc=1, device_id=where, device_id_type=MESH)
    pl.semaphore_wait(barrier, n + m - 2)

    def spread(s, src, dst, offset):
        to = span(offset + place * rows, rows, rows)
        out = [
            remote(src, dst.at[to, :], r.sp_zs.at[s, k], r.sp_zr.at[s, k], column[k])
            for k in range(nz - 1)
        ]
        out.append(remote(src, dst.at[to, :], r.sp_xs.at[s, 0], r.sp_xr.at[s, 0], partner))
        for copy in out:
            copy.start()
        return out

    def forward(s, dst, offset, out):
        for k in range(1, nz):
            out[k - 1].wait_recv()
            at = span(offset + (xx * nz + lax.rem(zz + nz - k, nz)) * rows, rows, rows)
            copy = remote(
                dst.at[at, :], dst.at[at, :], r.sp_xs.at[s, k], r.sp_xr.at[s, k], partner
            )
            copy.start()
            out.append(copy)

    def arrived(out):
        for copy in out[nz - 1 :]:
            copy.wait_recv()

    token_copies = spread(0, r.tokens, r.xx, 0)
    task_copies = [
        remote(r.task_own, r.task_slots.at[k], r.task_s.at[k], r.task_r.at[k], dp_places[k])
        for k in range(n - 1)
    ]
    for copy in task_copies:
        copy.start()
    forward(0, r.xx, 0, token_copies)
    arrived(token_copies)
    for load in loads:
        load.wait()
    tokens = r.xx

    def first_hop(s, i):
        at = span(i * h, h, 16)
        return remote(
            r.part.at[s, at, :], r.got.at[s, at, :], r.ex_s.at[s, 0, i], r.ex_r.at[s, 0, i], flip(0)
        )

    def wire_hop(s, bit, i):
        at = span(i * h, h, 16)
        return remote(
            r.sent.at[s, bit - 1, at, :],
            r.wire.at[s, bit - 1, at, :],
            r.ex_s.at[s, bit, i],
            r.ex_r.at[s, bit, i],
            flip(bit),
        )

    full = [r.full.at[0], r.full.at[1], r.gate]

    def last_hop(s, i):
        at = span(mine + i * h, h, 16)
        return remote(
            full[s].at[at, :], full[s].at[at, :], r.ex_s.at[s, bits, i], r.ex_r.at[s, bits, i], flip(0)
        )

    def send_chunks(s, make):
        def own_half(i):
            at = span(i * h, h, 16)
            first_hop(s, i).wait_recv()
            value = (r.keep[at, :] + r.got[s, at, :].astype(F32)).astype(BF)
            if bits > 1:
                r.sent[s, 0, at, :] = value
                wire_hop(s, 1, i).start()
            else:
                r.part_own[at, :] = value

        def step(i, _):
            at = span(i * h, h, 16)
            r.part[s, at, :] = make(other + i * h).astype(BF)
            first_hop(s, i).start()
            r.keep[at, :] = make(mine + i * h)

            @pl.when(i > 0)
            def _():
                own_half(i - 1)

            return 0

        lax.fori_loop(0, STEPS, step, 0)
        own_half(STEPS - 1)

    def take_chunks(s, use, begin, end):
        def step(i, _):
            at = span(i * h, h, 16)
            for bit in range(1, bits):
                wire_hop(s, bit, i).wait_recv()
                value = r.sent[s, bit - 1, at, :].astype(F32) + r.wire[s, bit - 1, at, :].astype(F32)
                value = value.astype(BF)
                if bit + 1 < bits:
                    r.sent[s, bit, at, :] = value
                    wire_hop(s, bit + 1, i).start()
            full[s][span(mine + i * h, h, 16), :] = value
            last_hop(s, i).start()
            use(mine + i * h)
            last_hop(s, i).wait_recv()
            use(other + i * h)
            return 0

        lax.fori_loop(begin, end, step, 0)

    def linear_rows(kind):
        def make(row):
            return contract_last(r.w[kind, span(row, h, 16), :], tokens[...])

        return make

    def hidden_rows(row):
        at = span(row, h, 16)
        activation, derivative, second_order = sigmoid_parts(r.full[0, at, :])
        hidden = activation.astype(BF)
        r.both[at, count:] = hidden
        r.derivative[at, :] = derivative
        r.second[at, :] = second_order
        r.acc[0] += contract_first(hidden, r.w[2, at, :])
        r.acc[1] += contract_first(hidden, r.w[3, at, :])

    def tangent_rows(row):
        at = span(row, h, 16)
        tangent = (r.derivative[at, :] * r.full[1, at, :].astype(F32)).astype(BF)
        r.both[at, :count] = tangent
        r.acc[1] += contract_first(tangent, r.w[2, at, :])

    own_half_rows = span(xx * half, half, half)

    def reduce_start(s):
        r.half_out[s] = r.acc[s, span((1 - xx) * half, half, half), :].astype(BF)
        copy = remote(r.half_out.at[s], r.half_in.at[s], r.rx_s.at[s], r.rx_r.at[s], partner)
        copy.start()
        return [copy]

    def reduce_middle(s, out):
        out[0].wait_recv()
        value = r.acc[s, own_half_rows, :] + r.half_in[s].astype(F32)
        r.acc[s, own_half_rows, :] = value
        r.column_out[s] = value.astype(BF)
        for k in range(1, nz):
            copy = remote(
                r.column_out.at[s, span(lax.rem(zz + k, nz) * rows, rows, rows), :],
                r.column_in.at[s, k - 1],
                r.rz_s.at[s, k - 1],
                r.rz_r.at[s, k - 1],
                column[k - 1],
            )
            copy.start()
            out.append(copy)

    def reduce_end(s, out):
        value = r.acc[s, block, :]
        for k in range(1, nz):
            out[k].wait_recv()
            value = value + r.column_in[s, k - 1].astype(F32)
        return value

    k_mine, k_other = span(low * half, half, half), span((1 - low) * half, half, half)

    def gram_copy(j):
        if j == 0:
            src, dst = r.token_gram.at[k_other, :], r.gram_got
        elif j < bits:
            src, dst = r.gram_sent.at[j - 1], r.gram_wire.at[j - 1]
        else:
            src, dst = r.gram_full.at[k_mine, :], r.gram_full.at[k_mine, :]
        return remote(src, dst, r.gram_s.at[j], r.gram_r.at[j], flip(0 if j == bits else j))

    def gram_step(j):
        if j == 0:
            r.token_gram[...] = contract_last(tokens[...], tokens[...])
            gram_copy(0).start()
            return
        gram_copy(j - 1).wait_recv()
        if j == 1:
            value = r.token_gram[k_mine, :] + r.gram_got[...]
        elif j <= bits:
            value = r.gram_sent[j - 2] + r.gram_wire[j - 2]
        if j < bits:
            r.gram_sent[j - 1] = value
        elif j == bits:
            r.gram_full[k_mine, :] = value
        if j <= bits:
            gram_copy(j).start()
            return
        high = r.gram_full[...].astype(BF)
        r.gram_parts[0] = high
        r.gram_parts[1] = (r.gram_full[...] - high.astype(F32)).astype(BF)

    send_chunks(0, linear_rows(0))
    send_chunks(1, linear_rows(1))
    gram_step(0)
    take_chunks(0, hidden_rows, 0, STEPS)
    y_copies = reduce_start(0)
    gram_step(1)
    take_chunks(1, tangent_rows, 0, STEPS // 2)
    reduce_middle(0, y_copies)
    take_chunks(1, tangent_rows, STEPS // 2, STEPS)
    z_copies = reduce_start(1)
    for j in range(2, bits + 1):
        gram_step(j)

    same = jnp.where(own_row[0:1, :] == own_col, 1.0, 0.0)
    for k, copy in enumerate(task_copies):
        copy.wait_recv()
        same = same + jnp.where(r.task_slots[k, 0:1, :] == own_col, 1.0, 0.0)
    weight = 1.0 / (TASKS * jnp.sum(same, axis=1, keepdims=True))

    value = reduce_end(0, y_copies)
    r.fresh[0] = (weight * (value - r.targets[...].astype(F32))).astype(BF)
    r.ee[block, :] = r.fresh[0]
    e_copies = spread(1, r.fresh.at[0], r.ee, 0)
    reduce_middle(1, z_copies)

    def gram_rows(kind):
        at = span(kind * h, h, 16)
        r.both_gram[...] += contract_first(r.both[at, :], r.both[at, :])

    r.both_gram[...] = jnp.zeros(r.both_gram.shape, F32)
    lax.fori_loop(0, 2 * STEPS, lambda i, _: (gram_rows(i), 0)[1], 0)
    forward(1, r.ee, 0, e_copies)
    value = reduce_end(1, z_copies)
    first = summed(weight * (value * value))
    r.fresh[1] = (weight * value).astype(BF)
    r.ee[span(count + place * rows, rows, rows), :] = r.fresh[1]
    t_copies = spread(2, r.fresh.at[1], r.ee, count)
    arrived(e_copies)

    def error_rows(i, kept):
        at = span(i * h, h, 16)
        errors = r.ee[pl.ds(0, count), :]
        back = contract_last(r.w[2, at, :], errors)
        crossing = contract_last(r.w[3, at, :], errors)
        tangent = r.full[1, at, :].astype(F32)
        curved = r.second[at, :] * back
        r.curved[at, :] = curved
        r.gate_base[at, :] = r.derivative[at, :] * crossing + curved * tangent
        term = 2.0 * r.both[at, :count].astype(F32) * crossing + curved * tangent * tangent
        return kept + folded(term)

    kept = lax.fori_loop(0, 2 * STEPS, error_rows, jnp.zeros((8, count), F32))
    first = first * jnp.ones((1, 128), F32)
    first_part = summed(kept)
    gram_step(bits + 1)

    def norm_rows(i, kept):
        at = span(i * 16, 16, 16)
        one, two = r.w[1, at, :].astype(F32), r.w[3, at, :].astype(F32)
        return kept + one * one + two * two

    norm = summed(lax.fori_loop(0, total // 16, norm_rows, jnp.zeros((16, width), F32)))
    forward(2, r.ee, count, t_copies)
    arrived(t_copies)

    def gate_make(row):
        at = span(row, h, 16)
        back = contract_last(r.w[2, at, :], r.ee[pl.ds(count, count), :])
        return r.gate_base[at, :] + r.derivative[at, :] * back

    r.kept[...] = jnp.zeros(r.kept.shape, F32)
    r.gate_gram[...] = jnp.zeros(r.gate_gram.shape, F32)
    r.carry_gram[...] = jnp.zeros(r.carry_gram.shape, F32)

    def gate_rows(row):
        at = span(row, h, 16)
        gate = r.gate[at, :]
        lowered = product(gate, r.gram_parts[0]) + product(gate, r.gram_parts[1])
        carried = (r.derivative[at, :] * lowered).astype(BF)
        r.acc[2] += contract_first(carried, r.w[2, at, :])
        r.gate_gram[...] += contract_first(gate, gate)
        r.carry_gram[...] += contract_first(carried, r.both[at, :])
        r.kept[...] += folded(r.curved[at, :] * lowered * lowered)

    send_chunks(2, gate_make)
    take_chunks(2, gate_rows, 0, STEPS)
    head, tail = pl.ds(0, count), pl.ds(count, count)
    r.acc[2] += product(r.both_gram[tail, :].astype(BF), r.ee[...])
    w_copies = reduce_start(2)

    gram = contract_last(r.ee[...], r.ee[...])
    h_t = summed(r.both_gram[tail, head] * gram[count:, :count])
    change = summed(r.gate_gram[...] * r.token_gram[...]) + 2.0 * h_t
    change = change + summed(r.both_gram[head, head] * gram[:count, :count])
    change = change + summed(r.both_gram[tail, tail] * gram[count:, count:])
    carry = summed(r.carry_gram[:, head] * gram[:count, :count])
    carry = carry + summed(r.carry_gram[:, tail] * gram[:count, count:])
    final = summed(r.kept[...]) + 2.0 * carry

    reduce_middle(2, w_copies)
    value = reduce_end(2, w_copies)
    final = final + summed(weight * (value * value))
    index = lax.broadcasted_iota(jnp.int32, (8, 128), 0)
    value = jnp.zeros((8, 128), F32)
    for at, number in enumerate((norm, first + first_part, change, final)):
        value = value + jnp.where(index == at, number, 0.0)
    r.own[0] = value
    dp_copies = [
        remote(r.own.at[0], r.dp_slots.at[k], r.dp_s.at[k], r.dp_r.at[k], dp_places[k])
        for k in range(n - 1)
    ]
    for copy in dp_copies:
        copy.start()
    for k, copy in enumerate(dp_copies):
        copy.wait_recv()
        value = value + r.dp_slots[k]
    r.own[1] = value
    shard_copies = [
        remote(r.own.at[1], r.shard_slots.at[k], r.sh_s.at[k], r.sh_r.at[k], shard_places[k])
        for k in range(m - 1)
    ]
    for copy in shard_copies:
        copy.start()
    for k, copy in enumerate(shard_copies):
        copy.wait_recv()
        value = value + r.shard_slots[k]
    r.own[2] = value
    norm, first, change, final = (r.own[2, i : i + 1, :] for i in range(4))
    step = norm / (norm + first)
    keep = first / (norm + first)
    norm_next = keep * keep * norm - 2.0 * keep * step * first + step * step * change
    ratio = norm_next / norm
    curvature = (
        norm_next
        + keep * keep * first
        - 2.0 * keep * step * change
        + step * step * final
        - ratio * norm_next / step
    )
    step_next = norm_next / curvature
    r.sums[0:1, :] = step + step_next * (ratio + keep)
    r.sums[1:2, :] = -step_next * step

    def sends_done(i, _):
        for s in range(3):
            first_hop(s, i).wait_send()
            for bit in range(1, bits):
                wire_hop(s, bit, i).wait_send()
            last_hop(s, i).wait_send()
        return 0

    lax.fori_loop(0, STEPS, sends_done, 0)
    for j in range(bits + 1):
        gram_copy(j).wait_send()
    for copy in token_copies + e_copies + t_copies + y_copies + z_copies + w_copies:
        copy.wait_send()
    for copy in task_copies + dp_copies + shard_copies:
        copy.wait_send()


def fused(n, m, tokens, targets, task, up, outer_up, down, outer_down):
    hid, width = up.shape
    rows = tokens.shape[0]
    count, half, nz = n * rows, n * rows // 2, n // 2
    bits = m.bit_length() - 1
    hp = -(-hid // (2 * 16 * STEPS)) * 16 * STEPS
    total = 2 * hp
    vm, dma = pltpu.VMEM, pltpu.SemaphoreType.DMA
    links = max(bits - 1, 1)
    outs = {
        "gate": ((total, count), BF),
        "both": ((total, 2 * count), BF),
        "xx": ((count, width), BF),
        "ee": ((2 * count, width), BF),
        "sums": ((8, 128), F32),
    }
    scratch = {
        "w": vm((4, total, width), BF),
        "part": vm((3, hp, count), BF),
        "keep": vm((hp, count), F32),
        "got": vm((3, hp, count), BF),
        "sent": vm((3, links, hp, count), BF),
        "wire": vm((3, links, hp, count), BF),
        "full": vm((2, total, count), BF),
        "derivative": vm((total, count), F32),
        "second": vm((total, count), F32),
        "curved": vm((total, count), F32),
        "gate_base": vm((total, count), F32),
        "acc": vm((3, count, width), F32),
        "half_out": vm((3, half, width), BF),
        "half_in": vm((3, half, width), BF),
        "column_out": vm((3, half, width), BF),
        "column_in": vm((3, nz - 1, rows, width), BF),
        "fresh": vm((2, rows, width), BF),
        "token_gram": vm((count, count), F32),
        "gram_got": vm((half, count), F32),
        "gram_sent": vm((links, half, count), F32),
        "gram_wire": vm((links, half, count), F32),
        "gram_full": vm((count, count), F32),
        "gram_parts": vm((2, count, count), BF),
        "both_gram": vm((2 * count, 2 * count), F32),
        "gate_gram": vm((count, count), F32),
        "carry_gram": vm((count, 2 * count), F32),
        "kept": vm((8, count), F32),
        "task_own": vm((8, 128), F32),
        "task_slots": vm((n - 1, 8, 128), F32),
        "own": vm((3, 8, 128), F32),
        "dp_slots": vm((n - 1, 8, 128), F32),
        "shard_slots": vm((m - 1, 8, 128), F32),
        "load_sem": dma((4,)),
        "task_s": dma((n - 1,)),
        "task_r": dma((n - 1,)),
        "sp_zs": dma((3, nz - 1)),
        "sp_zr": dma((3, nz - 1)),
        "sp_xs": dma((3, nz)),
        "sp_xr": dma((3, nz)),
        "ex_s": dma((3, bits + 1, STEPS)),
        "ex_r": dma((3, bits + 1, STEPS)),
        "rx_s": dma((3,)),
        "rx_r": dma((3,)),
        "rz_s": dma((3, nz - 1)),
        "rz_r": dma((3, nz - 1)),
        "gram_s": dma((bits + 1,)),
        "gram_r": dma((bits + 1,)),
        "dp_s": dma((n - 1,)),
        "dp_r": dma((n - 1,)),
        "sh_s": dma((m - 1,)),
        "sh_r": dma((m - 1,)),
    }
    inputs = ("task", "tokens", "targets", "up", "outer_up", "down", "outer_down")
    whole = pl.BlockSpec(memory_space=pltpu.VMEM)
    return pl.pallas_call(
        functools.partial(fused_kernel, n, m, hid, inputs + tuple(outs) + tuple(scratch)),
        out_shape=[jax.ShapeDtypeStruct(*o) for o in outs.values()],
        in_specs=[pl.BlockSpec(memory_space=pltpu.SMEM), whole, whole]
        + [pl.BlockSpec(memory_space=pl.ANY)] * 4,
        out_specs=[whole] * len(outs),
        scratch_shapes=list(scratch.values()),
        compiler_params=pltpu.CompilerParams(
            collective_id=0, has_side_effects=True, vmem_limit_bytes=VMEM_LIMIT
        ),
    )(task, tokens, targets, up, outer_up, down, outer_down)


def output_kernel(sums, gate, both, xx, ee, outer_up, outer_down, meta_up, meta_down):
    of_outer, of_change = sums[0:1, 0:1], sums[1:2, 0:1]
    meta_up[...] = of_outer * outer_up[...].astype(F32) + of_change * product(gate[...], xx[...])
    change = product(both[...], ee[...])
    meta_down[...] = of_outer * outer_down[...].astype(F32) + of_change * change


def outputs(gate, both, xx, ee, sums, outer_up, outer_down):
    hid, width = outer_up.shape
    tile = max(t for t in range(16, 601, 16) if hid % t == 0)

    def tiled(columns):
        return pl.BlockSpec((tile, columns), lambda i: (i, 0))

    def whole(array):
        return pl.BlockSpec(array.shape, lambda i: (0, 0))

    return pl.pallas_call(
        output_kernel,
        grid=(hid // tile,),
        out_shape=[jax.ShapeDtypeStruct((hid, width), F32)] * 2,
        in_specs=[
            whole(sums), tiled(gate.shape[1]), tiled(both.shape[1]), whole(xx), whole(ee),
            tiled(width), tiled(width),
        ],
        out_specs=[tiled(width)] * 2,
    )(sums, gate, both, xx, ee, outer_up, outer_down)


def body(n, m, tokens, targets, task_of_token, up_weight, down_weight, outer_up, outer_down):
    gate, both, xx, ee, sums = fused(
        n, m, tokens, targets, task_of_token, up_weight, outer_up, down_weight, outer_down
    )
    return tuple(outputs(gate, both, xx, ee, sums, outer_up, outer_down))


def solution(mesh):
    placed = tuple(P("dp") if i == 2 else P("dp", "shard") for i in range(7))
    return jax.shard_map(
        functools.partial(body, mesh.shape["dp"], mesh.shape["shard"]),
        mesh=mesh,
        in_specs=placed,
        out_specs=(P("dp", "shard"), P("dp", "shard")),
        check_vma=False,
    )
```

time: 132 us -> 99.2 us (0.75)
  matrix products: 32.8 us -> 0 us
  Pallas kernels: 89.8 us -> 98.4 us
  local copies, waits for them, and re-layouts: 4.57 us -> 0 us
  other arithmetic: 3.38 us -> 0 us
    dot_general x16 -> x0, matrix products: 32.8 us -> none  [the longest x2 12.6 us: contract_first(): lax.dot_general(left_side, right_side, (((0,), (0,)), ((), ())), preferre...]
    pallas_call x5 -> x2, Pallas kernels: 89.8 us -> 98.4 us  [the longest x1 88 us: fused(): pl.pallas_call(functools.partial(fused_kernel, n, m, hid, inputs + tuple(...]
    unnamed x19 -> x0, local copies, waits for them, and re-layouts: 3.02 us -> none
    add x1 -> x0, other arithmetic: 1.92 us -> none  [body(): part = part + jnp.where(index == place, value, 0.0)]
where the time goes in v1:
time: 99.2 us; the launch traced here: 99 us
  Pallas kernels  98.4 us (99%)
    pallas_call x1, Pallas kernels, fused(): pl.pallas_call(functools.partial(fused_kernel, n, m, hid, inputs + tuple(...  88 us
    pallas_call x1, Pallas kernels, outputs(): pl.pallas_call(output_kernel, grid=(hid // tile,), out_shape=[jax.ShapeDt...  10.4 us

profile of v1, /device:TPU:0, one launch (start us, length us, event | category | flops | bytes accessed | tf_op | source)
XLA Modules:
  0.0 99.0 jit_solution(10112379171804710416)
XLA Ops:
  0.6 88.0 %shard_map.86 = (bf16[2432,128]{1,0:T(8,128)(2,1)}, bf16[2432,256]{1,0:T(8,128)(2,1)}, bf16[128,896]{1,0:T(8,128)(2,1)}, bf16[256,896]{1,0:T(8,128)(2,1)}, f32[8,128]{1,0:T(8,128)}) custom-call(s32[16]{0:T(128)} %refs_0_.1, bf16[16,896]{1,0:T(8,128)(2,1)} %refs_1_.1, bf16[16,896]{1,0:T(8,128)(2,1)} %refs_2_.1, bf16[2368,896]{1,0:T(8,128)(2,1)} %refs_3_.1, ...), custom_call_target="tpu_custom_call" | custom-call | tf_op jit(solution)/shard_map/pallas_call | solution.py:539
  88.6 10.4 %shard_map.87 = (f32[2368,896]{1,0:T(8,128)}, f32[2368,896]{1,0:T(8,128)}) custom-call(f32[8,128]{1,0:T(8,128)} %get-tuple-element.7.sums, bf16[2432,128]{1,0:T(8,128)(2,1)} %get-tuple-element.8.gate, bf16[2432,256]{1,0:T(8,128)(2,1)} %get-tuple-element.9.both, bf16[128,896]{1,0:T(8,128)(2,1)} %get-tuple-element.10.xx, ...), custom_call_target="tpu_custom_call" | custom-call | tf_op jit(solution)/shard_map/pallas_call | solution.py:569

commit v2 on v1

v2 whole, which is shorter than its diff:
```python
import functools
import types

import jax
import jax.numpy as jnp
from jax import lax
from jax.experimental import pallas as pl
from jax.experimental.pallas import tpu as pltpu
from jax.sharding import PartitionSpec as P

TASKS = 16
STEPS = 4
BF = jnp.bfloat16
F32 = jnp.float32
MESH = pl.DeviceIdType.MESH
VMEM_LIMIT = 44 * 2**20
OUT_LIMIT = 24 * 2**20


def sigmoid_parts(linear_part):
    argument = linear_part.astype(F32)
    logistic = jax.nn.sigmoid(argument)
    derivative = logistic * (1.0 + argument * (1.0 - logistic))
    second_order = logistic * (1.0 - logistic) * (2.0 + argument * (1.0 - 2.0 * logistic))
    return (argument * logistic, derivative, second_order)


def contract_last(left_side, right_side):
    return lax.dot_general(
        left_side, right_side, (((1,), (1,)), ((), ())), preferred_element_type=F32
    )


def contract_first(left_side, right_side):
    return lax.dot_general(
        left_side, right_side, (((0,), (0,)), ((), ())), preferred_element_type=F32
    )


def product(left_side, right_side):
    return jnp.dot(left_side, right_side, preferred_element_type=F32)


def remote(src, dst, send_sem, recv_sem, where):
    return pltpu.make_async_remote_copy(
        src_ref=src,
        dst_ref=dst,
        send_sem=send_sem,
        recv_sem=recv_sem,
        device_id=where,
        device_id_type=MESH,
    )


def summed(term):
    return jnp.sum(jnp.sum(term, axis=1, keepdims=True), axis=0, keepdims=True)


def folded(term):
    return jnp.sum(term.reshape(term.shape[0] // 8, 8, term.shape[1]), axis=0)


def span(start, size, unit):
    return pl.ds(pl.multiple_of(start, unit), size)


def fused_kernel(n, m, hid, names, *refs):
    r = types.SimpleNamespace(**dict(zip(names, refs)))
    rows, width = r.tokens_in.shape
    count, half, nz = n * rows, n * rows // 2, n // 2
    total = r.both.shape[0]
    hp = total // 2
    h = hp // STEPS
    wide = 2 * h
    bits = m.bit_length() - 1
    me = lax.axis_index("dp")
    xx, zz = lax.rem(me, 2), me // 2
    shard = lax.axis_index("shard")
    low = lax.rem(shard, 2)
    partner = {"dp": 2 * zz + 1 - xx}

    def across(j):
        to = zz
        for bit in range(nz.bit_length() - 1):
            if j >> bit & 1:
                step = 1 << bit
                to = to + step - 2 * step * lax.rem(zz // step, 2)
        return to

    column = [{"dp": 2 * across(j) + xx} for j in range(nz)]
    far_first = range(nz - 1, 0, -1)
    dp_places = [{"dp": lax.rem(me + k, n)} for k in range(1, n)]
    shard_places = [{"shard": lax.rem(shard + k, m)} for k in range(1, m)]
    all_places = [
        {"dp": lax.rem(me + a, n), "shard": lax.rem(shard + b, m)}
        for a in range(n)
        for b in range(m)
        if a + b
    ]

    def flip(bit):
        step = 1 << bit
        return {"shard": shard + step - 2 * step * lax.rem(shard // step, 2)}

    barrier = pltpu.get_barrier_semaphore()
    for where in all_places:
        pl.semaphore_signal(barrier, inc=1, device_id=where, device_id_type=MESH)
    small = [
        pltpu.make_async_copy(src, dst, r.small_sem.at[i])
        for i, (src, dst) in enumerate(
            ((r.task_in, r.task), (r.tokens_in, r.tokens), (r.targets_in, r.targets))
        )
    ]
    small[1].start()
    small[0].start()

    def load(src, dst, step, index):
        size = min(wide, hid - step * wide)
        return pltpu.make_async_copy(
            src.at[pl.ds(step * wide, size)], dst.at[pl.ds(0, size)], r.load_sem.at[index, step]
        )

    loads = []
    for step in range(STEPS):
        if step * wide < hid:
            loads.append(load(r.up, r.ups.at[step, 0], step, 0))
            loads.append(load(r.outer_up, r.ups.at[step, 1], step, 1))
    for step in range(STEPS):
        if step * wide < hid:
            loads.append(load(r.down, r.low_down.at[pl.ds(step * wide, wide)], step, 2))
            loads.append(load(r.outer_down, r.outer_low.at[pl.ds(step * wide, wide)], step, 3))
    small[1].wait()
    small[0].wait()
    for copy in loads + small[2:]:
        copy.start()

    block = span(zz * rows, rows, rows)
    r.xx[block, :] = r.tokens[...]
    for step in range(STEPS):
        gap = min(wide, (step + 1) * wide - hid)
        if gap > 0:
            r.ups[step, :, pl.ds(wide - gap, gap), :] = jnp.zeros((2, gap, width), BF)
    if total > hid:
        r.low_down[pl.ds(hid, total - hid), :] = jnp.zeros((total - hid, width), BF)
        r.outer_low[pl.ds(hid, total - hid), :] = jnp.zeros((total - hid, width), BF)
    r.acc[...] = jnp.zeros(r.acc.shape, F32)

    pl.semaphore_wait(barrier, n * m - 1)

    def spread(s, src, dst, offset):
        near = span(offset + zz * rows, rows, rows)
        over = span(offset + half + zz * rows, rows, rows)
        out = [
            remote(src, dst.at[near, :], r.sp_zs.at[s, j - 1], r.sp_zr.at[s, j - 1], column[j])
            for j in far_first
        ]
        out.append(remote(src, dst.at[over, :], r.sp_xs.at[s, 0], r.sp_xr.at[s, 0], partner))
        for copy in out:
            copy.start()
        return out

    def forward(s, dst, offset, out):
        for j in range(1, nz):
            out[nz - 1 - j].wait_recv()
            at = span(offset + across(j) * rows, rows, rows)
            over = span(offset + half + across(j) * rows, rows, rows)
            copy = remote(
                dst.at[at, :], dst.at[over, :], r.sp_xs.at[s, j], r.sp_xr.at[s, j], partner
            )
            copy.start()
            out.append(copy)

    def arrived(out):
        for copy in out[nz - 1 :]:
            copy.wait_recv()

    token_copies = spread(0, r.tokens, r.xx, 0)

    lane = lax.broadcasted_iota(jnp.int32, (8, 128), 1)
    line = lax.broadcasted_iota(jnp.int32, (rows, 128), 0)
    own_row = jnp.full((8, 128), -1.0, F32)
    own_col = jnp.zeros((rows, 128), F32)
    for i in range(rows):
        number = r.task[i].astype(F32)
        own_row = jnp.where(lane == i, number, own_row)
        own_col = jnp.where(line == i, number, own_col)
    r.task_own[...] = own_row
    task_copies = [
        remote(r.task_own, r.task_slots.at[k], r.task_s.at[k], r.task_r.at[k], dp_places[k])
        for k in range(n - 1)
    ]
    for copy in task_copies:
        copy.start()
    forward(0, r.xx, 0, token_copies)
    arrived(token_copies)
    for copy in loads + small[2:]:
        copy.wait()
    tokens = r.xx

    def chunk(i):
        return span(i * wide, wide, 16)

    def own_part(i):
        return span(i * wide + low * h, h, 16)

    def strip(i):
        return span(i * h, h, 16)

    full = [r.full.at[0], r.full.at[1], r.gate]

    def first_hop(s, i):
        away = span(i * wide + (1 - low) * h, h, 16)
        return remote(
            r.part.at[s, away, :], r.got.at[s, strip(i), :], r.ex_s.at[s, 0, i], r.ex_r.at[s, 0, i], flip(0)
        )

    def wire_hop(s, bit, i):
        return remote(
            r.sent.at[s, bit - 1, strip(i), :],
            r.wire.at[s, bit - 1, strip(i), :],
            r.ex_s.at[s, bit, i],
            r.ex_r.at[s, bit, i],
            flip(bit),
        )

    def last_hop(s, i):
        at = own_part(i)
        return remote(
            full[s].at[at, :], full[s].at[at, :], r.ex_s.at[s, bits, i], r.ex_r.at[s, bits, i], flip(0)
        )

    def pair_sum(s, i):
        first_hop(s, i).wait_recv()
        value = r.part[s, own_part(i), :].astype(F32) + r.got[s, strip(i), :].astype(F32)
        r.sent[s, 0, strip(i), :] = value.astype(BF)
        wire_hop(s, 1, i).start()

    def take_chunks(s, use, begin, end):
        def step(i, _):
            for bit in range(1, bits):
                wire_hop(s, bit, i).wait_recv()
                value = r.sent[s, bit - 1, strip(i), :].astype(F32)
                value = (value + r.wire[s, bit - 1, strip(i), :].astype(F32)).astype(BF)
                if bit + 1 < bits:
                    r.sent[s, bit, strip(i), :] = value
                    wire_hop(s, bit + 1, i).start()
            full[s][own_part(i), :] = value
            last_hop(s, i).start()

            @pl.when(i > 0)
            def _():
                last_hop(s, i - 1).wait_recv()
                use(chunk(i - 1))

            return 0

        lax.fori_loop(begin, end, step, 0)
        if end == STEPS:
            use(own_part(STEPS - 1))
            last_hop(s, STEPS - 1).wait_recv()
            use(span((STEPS - 1) * wide + (1 - low) * h, h, 16))

    def linear_step(i, _):
        value = contract_last(r.ups[i].reshape(2 * wide, width), tokens[...])
        for s in range(2):
            r.part[s, chunk(i), :] = value[s * wide : (s + 1) * wide].astype(BF)
            first_hop(s, i).start()

        @pl.when(i > 0)
        def _():
            pair_sum(0, i - 1)

        return 0

    def hidden_rows(at):
        activation, derivative, second_order = sigmoid_parts(r.full[0, at, :])
        hidden = activation.astype(BF)
        r.both[at, count:] = hidden
        r.derivative[at, :] = derivative
        r.second[at, :] = second_order
        r.acc[0] += contract_first(hidden, r.low_down[at, :])
        r.acc[1] += contract_first(hidden, r.outer_low[at, :])

    def tangent_rows(at):
        tangent = (r.derivative[at, :] * r.full[1, at, :].astype(F32)).astype(BF)
        r.both[at, :count] = tangent
        r.acc[1] += contract_first(tangent, r.low_down[at, :])

    def half_place(j):
        return span(across(j) * rows, rows, rows)

    def half_copy(s, j):
        return remote(
            r.half_out.at[s, half_place(j), :], r.half_in.at[s, j], r.rx_s.at[s, j], r.rx_r.at[s, j], partner
        )

    def column_copy(s, j):
        return remote(
            r.column_out.at[s, j - 1], r.column_in.at[s, j - 1], r.rz_s.at[s, j - 1], r.rz_r.at[s, j - 1], column[j]
        )

    def reduce_start(s):
        r.half_out[s] = r.acc[s, pl.ds(half, half), :].astype(BF)
        for j in range(nz - 1, -1, -1):
            half_copy(s, j).start()

    def pair_rows(s, j):
        half_copy(s, j).wait_recv()
        return r.acc[s, half_place(j), :] + r.half_in[s, j].astype(F32)

    def reduce_middle(s):
        for j in far_first:
            r.column_out[s, j - 1] = pair_rows(s, j).astype(BF)
            column_copy(s, j).start()

    def reduce_end(s):
        value = pair_rows(s, 0)
        for j in range(1, nz):
            column_copy(s, j).wait_recv()
            value = value + r.column_in[s, j - 1].astype(F32)
        return value

    def reduce_sent(s):
        for j in range(nz):
            half_copy(s, j).wait_send()
            if j:
                column_copy(s, j).wait_send()

    k_mine, k_other = span(low * half, half, half), span((1 - low) * half, half, half)

    def gram_copy(j):
        if j == 0:
            src, dst = r.token_gram.at[k_other, :], r.gram_got
        elif j < bits:
            src, dst = r.gram_sent.at[j - 1], r.gram_wire.at[j - 1]
        else:
            src, dst = r.gram_full.at[k_mine, :], r.gram_full.at[k_mine, :]
        return remote(src, dst, r.gram_s.at[j], r.gram_r.at[j], flip(0 if j == bits else j))

    def gram_step(j):
        if j == 0:
            r.token_gram[...] = contract_last(tokens[...], tokens[...])
            gram_copy(0).start()
            return
        gram_copy(j - 1).wait_recv()
        if j == 1:
            value = r.token_gram[k_mine, :] + r.gram_got[...]
        elif j <= bits:
            value = r.gram_sent[j - 2] + r.gram_wire[j - 2]
        if j < bits:
            r.gram_sent[j - 1] = value
        elif j == bits:
            r.gram_full[k_mine, :] = value
        if j <= bits:
            gram_copy(j).start()
            return
        high = r.gram_full[...].astype(BF)
        r.gram_parts[0] = high
        r.gram_parts[1] = (r.gram_full[...] - high.astype(F32)).astype(BF)

    lax.fori_loop(0, STEPS, linear_step, 0)
    pair_sum(0, STEPS - 1)
    lax.fori_loop(0, STEPS, lambda i, _: (pair_sum(1, i), 0)[1], 0)
    gram_step(0)
    take_chunks(0, hidden_rows, 0, STEPS)
    reduce_start(0)
    gram_step(1)
    take_chunks(1, tangent_rows, 0, STEPS - 1)
    reduce_middle(0)
    take_chunks(1, tangent_rows, STEPS - 1, STEPS)
    reduce_start(1)
    for j in range(2, bits + 1):
        gram_step(j)

    same = jnp.where(own_row[0:1, :] == own_col, 1.0, 0.0)
    for k, copy in enumerate(task_copies):
        copy.wait_recv()
        same = same + jnp.where(r.task_slots[k, 0:1, :] == own_col, 1.0, 0.0)
    weight = 1.0 / (TASKS * jnp.sum(same, axis=1, keepdims=True))

    value = reduce_end(0)
    r.fresh[0] = (weight * (value - r.targets[...].astype(F32))).astype(BF)
    r.ee[block, :] = r.fresh[0]
    e_copies = spread(1, r.fresh.at[0], r.ee, 0)
    reduce_middle(1)

    def gram_rows(i, _):
        at = chunk(i)
        r.both_gram[...] += contract_first(r.both[at, :], r.both[at, :])
        return 0

    r.both_gram[...] = jnp.zeros(r.both_gram.shape, F32)
    lax.fori_loop(0, STEPS, gram_rows, 0)
    forward(1, r.ee, 0, e_copies)
    value = reduce_end(1)
    first = summed(weight * (value * value))
    r.fresh[1] = (weight * value).astype(BF)
    r.ee[span(count + zz * rows, rows, rows), :] = r.fresh[1]
    t_copies = spread(2, r.fresh.at[1], r.ee, count)
    arrived(e_copies)

    def error_rows(i, kept):
        at = chunk(i)
        errors = r.ee[pl.ds(0, count), :]
        back = contract_last(r.low_down[at, :], errors)
        crossing = contract_last(r.outer_low[at, :], errors)
        tangent = r.full[1, at, :].astype(F32)
        curved = r.second[at, :] * back
        r.curved[at, :] = curved
        r.gate_base[at, :] = r.derivative[at, :] * crossing + curved * tangent
        term = 2.0 * r.both[at, :count].astype(F32) * crossing + curved * tangent * tangent
        return kept + folded(term)

    kept = lax.fori_loop(0, STEPS, error_rows, jnp.zeros((8, count), F32))
    first_part = summed(kept)
    gram_step(bits + 1)

    forward(2, r.ee, count, t_copies)
    def norm_rows(i, kept):
        for step in range(STEPS):
            one = r.ups[step, 1, span(i * 16, 16, 16), :].astype(F32)
            two = r.outer_low[span(step * wide + i * 16, 16, 16), :].astype(F32)
            kept = kept + one * one + two * two
        return kept

    norm = summed(lax.fori_loop(0, wide // 16, norm_rows, jnp.zeros((16, width), F32)))
    arrived(t_copies)

    def gate_step(i, _):
        at = chunk(i)
        back = contract_last(r.low_down[at, :], r.ee[pl.ds(count, count), :])
        r.part[2, at, :] = (r.gate_base[at, :] + r.derivative[at, :] * back).astype(BF)
        first_hop(2, i).start()

        @pl.when(i > 0)
        def _():
            pair_sum(2, i - 1)

        return 0

    r.kept[...] = jnp.zeros(r.kept.shape, F32)
    r.gate_gram[...] = jnp.zeros(r.gate_gram.shape, F32)
    r.carry_gram[...] = jnp.zeros(r.carry_gram.shape, F32)

    def gate_rows(at):
        gate = r.gate[at, :]
        lowered = product(gate, r.gram_parts[0]) + product(gate, r.gram_parts[1])
        carried = (r.derivative[at, :] * lowered).astype(BF)
        r.acc[2] += contract_first(carried, r.low_down[at, :])
        r.gate_gram[...] += contract_first(gate, gate)
        r.carry_gram[...] += contract_first(carried, r.both[at, :])
        r.kept[...] += folded(r.curved[at, :] * lowered * lowered)

    lax.fori_loop(0, STEPS, gate_step, 0)
    pair_sum(2, STEPS - 1)
    take_chunks(2, gate_rows, 0, STEPS)
    head, tail = pl.ds(0, count), pl.ds(count, count)
    r.acc[2] += product(r.both_gram[tail, :].astype(BF), r.ee[...])
    reduce_start(2)

    gram = contract_last(r.ee[...], r.ee[...])
    h_t = summed(r.both_gram[tail, head] * gram[count:, :count])
    change = summed(r.gate_gram[...] * r.token_gram[...]) + 2.0 * h_t
    change = change + summed(r.both_gram[head, head] * gram[:count, :count])
    change = change + summed(r.both_gram[tail, tail] * gram[count:, count:])
    carry = summed(r.carry_gram[:, head] * gram[:count, :count])
    carry = carry + summed(r.carry_gram[:, tail] * gram[:count, count:])
    final = summed(r.kept[...]) + 2.0 * carry

    reduce_middle(2)
    value = reduce_end(2)
    final = final + summed(weight * (value * value))
    index = lax.broadcasted_iota(jnp.int32, (1, 128), 1)
    value = jnp.zeros((1, 128), F32)
    for at, number in enumerate((norm, first + first_part, change, final)):
        value = value + jnp.where(index == at, number, 0.0)
    r.own[...] = value
    number_copies = [
        remote(r.own, r.slots.at[k], r.all_s.at[k], r.all_r.at[k], all_places[k])
        for k in range(n * m - 1)
    ]
    for copy in number_copies:
        copy.start()
    for k, copy in enumerate(number_copies):
        copy.wait_recv()
        value = value + r.slots[k]
    norm, first, change, final = (summed(jnp.where(index == at, value, 0.0)) for at in range(4))
    step = norm / (norm + first)
    keep = first / (norm + first)
    norm_next = keep * keep * norm - 2.0 * keep * step * first + step * step * change
    ratio = norm_next / norm
    curvature = (
        norm_next
        + keep * keep * first
        - 2.0 * keep * step * change
        + step * step * final
        - ratio * norm_next / step
    )
    step_next = norm_next / curvature
    r.sums[0:1, :] = jnp.broadcast_to(step + step_next * (ratio + keep), (1, 128))
    r.sums[1:2, :] = jnp.broadcast_to(-step_next * step, (1, 128))

    def sends_done(i, _):
        for s in range(3):
            first_hop(s, i).wait_send()
            for bit in range(1, bits):
                wire_hop(s, bit, i).wait_send()
            last_hop(s, i).wait_send()
        return 0

    lax.fori_loop(0, STEPS, sends_done, 0)
    for j in range(bits + 1):
        gram_copy(j).wait_send()
    for copy in token_copies + e_copies + t_copies + task_copies + number_copies:
        copy.wait_send()
    for s in range(3):
        reduce_sent(s)


def fused(n, m, tokens, targets, task, up, outer_up, down, outer_down):
    hid, width = up.shape
    rows = tokens.shape[0]
    count, half, nz = n * rows, n * rows // 2, n // 2
    bits = m.bit_length() - 1
    hp = -(-hid // (2 * 16 * STEPS)) * 16 * STEPS
    total = 2 * hp
    vm, dma = pltpu.VMEM, pltpu.SemaphoreType.DMA
    links = max(bits - 1, 1)
    outs = {
        "gate": ((total, count), BF),
        "both": ((total, 2 * count), BF),
        "xx": ((count, width), BF),
        "ee": ((2 * count, width), BF),
        "ups": ((STEPS, 2, total // STEPS, width), BF),
        "outer_low": ((total, width), BF),
        "sums": ((8, 128), F32),
    }
    scratch = {
        "low_down": vm((total, width), BF),
        "part": vm((3, total, count), BF),
        "got": vm((3, hp, count), BF),
        "sent": vm((3, links, hp, count), BF),
        "wire": vm((3, links, hp, count), BF),
        "full": vm((2, total, count), BF),
        "derivative": vm((total, count), F32),
        "second": vm((total, count), F32),
        "curved": vm((total, count), F32),
        "gate_base": vm((total, count), F32),
        "acc": vm((3, count, width), F32),
        "half_out": vm((3, half, width), BF),
        "half_in": vm((3, nz, rows, width), BF),
        "column_out": vm((3, nz - 1, rows, width), BF),
        "column_in": vm((3, nz - 1, rows, width), BF),
        "fresh": vm((2, rows, width), BF),
        "token_gram": vm((count, count), F32),
        "gram_got": vm((half, count), F32),
        "gram_sent": vm((links, half, count), F32),
        "gram_wire": vm((links, half, count), F32),
        "gram_full": vm((count, count), F32),
        "gram_parts": vm((2, count, count), BF),
        "both_gram": vm((2 * count, 2 * count), F32),
        "gate_gram": vm((count, count), F32),
        "carry_gram": vm((count, 2 * count), F32),
        "kept": vm((8, count), F32),
        "tokens": vm(tokens.shape, BF),
        "targets": vm(targets.shape, BF),
        "task": pltpu.SMEM(task.shape, task.dtype),
        "task_own": vm((8, 128), F32),
        "task_slots": vm((n - 1, 8, 128), F32),
        "own": vm((1, 128), F32),
        "slots": vm((n * m - 1, 1, 128), F32),
        "small_sem": dma((3,)),
        "load_sem": dma((4, STEPS)),
        "task_s": dma((n - 1,)),
        "task_r": dma((n - 1,)),
        "sp_zs": dma((3, nz - 1)),
        "sp_zr": dma((3, nz - 1)),
        "sp_xs": dma((3, nz)),
        "sp_xr": dma((3, nz)),
        "ex_s": dma((3, bits + 1, STEPS)),
        "ex_r": dma((3, bits + 1, STEPS)),
        "rx_s": dma((3, nz)),
        "rx_r": dma((3, nz)),
        "rz_s": dma((3, nz - 1)),
        "rz_r": dma((3, nz - 1)),
        "gram_s": dma((bits + 1,)),
        "gram_r": dma((bits + 1,)),
        "all_s": dma((n * m - 1,)),
        "all_r": dma((n * m - 1,)),
    }
    inputs = ("task_in", "tokens_in", "targets_in", "up", "outer_up", "down", "outer_down")
    arrays = (task, tokens, targets, up, outer_up, down, outer_down)
    whole = pl.BlockSpec(memory_space=pltpu.VMEM)
    return pl.pallas_call(
        functools.partial(fused_kernel, n, m, hid, inputs + tuple(outs) + tuple(scratch)),
        out_shape=[vm(*o) for o in outs.values()],
        in_specs=[pl.BlockSpec(memory_space=pltpu.HBM)] * len(inputs),
        out_specs=[whole] * len(outs),
        scratch_shapes=list(scratch.values()),
        compiler_params=pltpu.CompilerParams(
            collective_id=0, has_side_effects=True, vmem_limit_bytes=VMEM_LIMIT
        ),
    )(*(pltpu.with_memory_space_constraint(a, pltpu.HBM) for a in arrays))


def output_tiles(hid, wide):
    tiles, start = [], 0
    while start < hid:
        size = 64 if start == 0 else wide // 2
        size = min(size, wide - start % wide, hid - start)
        tiles.append((start, size))
        start += size
    return tiles


def output_kernel(
    gate, both, xx, ee, ups, outer_low, sums, meta_up, meta_down, stage, sems
):
    hid, width = meta_up.shape
    of_outer, of_change = sums[0:1, 0:1], sums[1:2, 0:1]
    wide = ups.shape[2]
    copies = []
    for i, (start, size) in enumerate(output_tiles(hid, wide)):
        at, part = pl.ds(start, size), pl.ds(start % wide, size)
        outer = ups[start // wide, 1, part, :].astype(F32)
        stage[0, at, :] = of_outer * outer + of_change * product(gate[at, :], xx[...])
        outer = outer_low[at, :].astype(F32)
        stage[1, at, :] = of_outer * outer + of_change * product(both[at, :], ee[...])
        for k, meta in enumerate((meta_up, meta_down)):
            copies.append(
                pltpu.make_async_copy(stage.at[k, at, :], meta.at[at, :], sems.at[k, i])
            )
            copies[-1].start()
    for copy in copies:
        copy.wait()


def outputs(hid, gate, both, xx, ee, ups, outer_low, sums):
    width = xx.shape[1]
    tiles = len(output_tiles(hid, ups.shape[2]))
    return pl.pallas_call(
        output_kernel,
        out_shape=[jax.ShapeDtypeStruct((hid, width), F32)] * 2,
        in_specs=[pl.BlockSpec(memory_space=pltpu.VMEM)] * 7,
        out_specs=[pl.BlockSpec(memory_space=pltpu.HBM)] * 2,
        scratch_shapes=[
            pltpu.VMEM((2, hid, width), F32),
            pltpu.SemaphoreType.DMA((2, tiles)),
        ],
        compiler_params=pltpu.CompilerParams(vmem_limit_bytes=OUT_LIMIT),
    )(gate, both, xx, ee, ups, outer_low, sums)


def body(n, m, tokens, targets, task_of_token, up_weight, down_weight, outer_up, outer_down):
    results = fused(
        n, m, tokens, targets, task_of_token, up_weight, outer_up, down_weight, outer_down
    )
    return tuple(outputs(up_weight.shape[0], *results))


def solution(mesh):
    placed = tuple(P("dp") if i == 2 else P("dp", "shard") for i in range(7))
    return jax.shard_map(
        functools.partial(body, mesh.shape["dp"], mesh.shape["shard"]),
        mesh=mesh,
        in_specs=placed,
        out_specs=(P("dp", "shard"), P("dp", "shard")),
        check_vma=False,
    )
```

time: 99.2 us -> 82.8 us (0.83)
  Pallas kernels: 98.4 us -> 82 us
    pallas_call x1, Pallas kernels: 88 us -> 75.5 us  [fused(): pl.pallas_call(functools.partial(fused_kernel, n, m, hid, inputs + tuple(...]
    pallas_call x1, Pallas kernels: 10.4 us -> 6.49 us  [outputs(): pl.pallas_call(output_kernel, out_shape=[jax.ShapeDtypeStruct((hid, width...]
where the time goes in v2:
time: 82.8 us; the launch traced here: 82.6 us
  Pallas kernels  82 us (99%)
    pallas_call x1, Pallas kernels, fused(): pl.pallas_call(functools.partial(fused_kernel, n, m, hid, inputs + tuple(...  75.5 us
    pallas_call x1, Pallas kernels, outputs(): pl.pallas_call(output_kernel, out_shape=[jax.ShapeDtypeStruct((hid, width...  6.49 us

profile of v2, /device:TPU:0, one launch (start us, length us, event | category | flops | bytes accessed | tf_op | source)
XLA Modules:
  0.0 82.6 jit_solution(1512036013995069605)
XLA Ops:
  0.6 75.5 %shard_map.86 = (bf16[2432,128]{1,0:T(8,128)(2,1)S(1)}, bf16[2432,256]{1,0:T(8,128)(2,1)S(1)}, bf16[128,896]{1,0:T(8,128)(2,1)S(1)}, bf16[256,896]{1,0:T(8,128)(...) custom-call(s32[16]{0:T(128)} %refs_0_.1, ...), custom_call_target="tpu_custom_call" | custom-call | tf_op jit(solution)/shard_map/pallas_call | solution.py:594
  76.1 6.5 %shard_map.87 = (f32[2368,896]{1,0:T(8,128)}, f32[2368,896]{1,0:T(8,128)}) custom-call(bf16[2432,128]{1,0:T(8,128)(2,1)S(1)} %get-tuple-element.9.gate, bf16[2432,256]{1,0:T(8,128)(2,1)S(1)} %get-tuple-element.10.both, bf16[128,896]{1,0:T(8,128)(2,1)S(1)} %get-tuple-element.11.xx, bf16[256,896]{1,0:T(8,128)(2,1)S(1)} %get-tuple-element.12.ee, ...), custom_call_target="tpu_custom_call" | custom-call | tf_op jit(solution)/shard_map/pallas_call | solution.py:641

commit v3 on v2

--- a/solution.py
+++ b/solution.py
@@ -79,6 +79,9 @@
     low = lax.rem(shard, 2)
     partner = {"dp": 2 * zz + 1 - xx}
 
+    def drain(ref, sem):
+        pltpu.make_async_copy(ref, ref, sem).wait()
+
     def across(j):
         to = zz
         for bit in range(nz.bit_length() - 1):
@@ -117,7 +120,7 @@
     def load(src, dst, step, index):
         size = min(wide, hid - step * wide)
         return pltpu.make_async_copy(
-            src.at[pl.ds(step * wide, size)], dst.at[pl.ds(0, size)], r.load_sem.at[index, step]
+            src.at[pl.ds(step * wide, size)], dst.at[pl.ds(0, size)], r.load_sem.at[index]
         )
 
     loads = []
@@ -151,10 +154,10 @@
         near = span(offset + zz * rows, rows, rows)
         over = span(offset + half + zz * rows, rows, rows)
         out = [
-            remote(src, dst.at[near, :], r.sp_zs.at[s, j - 1], r.sp_zr.at[s, j - 1], column[j])
+            remote(src, dst.at[near, :], r.sp_s.at[s], r.sp_zr.at[s, j - 1], column[j])
             for j in far_first
         ]
-        out.append(remote(src, dst.at[over, :], r.sp_xs.at[s, 0], r.sp_xr.at[s, 0], partner))
+        out.append(remote(src, dst.at[over, :], r.sp_s.at[s], r.sp_xr.at[s], partner))
         for copy in out:
             copy.start()
         return out
@@ -165,14 +168,12 @@
             at = span(offset + across(j) * rows, rows, rows)
             over = span(offset + half + across(j) * rows, rows, rows)
             copy = remote(
-                dst.at[at, :], dst.at[over, :], r.sp_xs.at[s, j], r.sp_xr.at[s, j], partner
+                dst.at[at, :], dst.at[over, :], r.sp_s.at[s], r.sp_xr.at[s], partner
             )
             copy.start()
-            out.append(copy)
-
-    def arrived(out):
-        for copy in out[nz - 1 :]:
-            copy.wait_recv()
+
+    def arrived(s):
+        drain(r.xx.at[pl.ds(0, half), :], r.sp_xr.at[s])
 
     token_copies = spread(0, r.tokens, r.xx, 0)
 
@@ -186,15 +187,16 @@
         own_col = jnp.where(line == i, number, own_col)
     r.task_own[...] = own_row
     task_copies = [
-        remote(r.task_own, r.task_slots.at[k], r.task_s.at[k], r.task_r.at[k], dp_places[k])
+        remote(r.task_own, r.task_slots.at[k], r.task_s, r.task_r, dp_places[k])
         for k in range(n - 1)
     ]
     for copy in task_copies:
         copy.start()
     forward(0, r.xx, 0, token_copies)
-    arrived(token_copies)
-    for copy in loads + small[2:]:
-        copy.wait()
+    arrived(0)
+    small[2].wait()
+    for i in range(4):
+        drain(r.low_down.at[pl.ds(0, hid), :], r.load_sem.at[i])
     tokens = r.xx
 
     def chunk(i):
@@ -206,19 +208,33 @@
     def strip(i):
         return span(i * h, h, 16)
 
-    full = [r.full.at[0], r.full.at[1], r.gate]
+    full = [r.full.at[0], r.full.at[1], r.full.at[2]]
+    pairs = STEPS // 2
+    lanes = [slice(0, half), slice(half, count)]
+
+    def side(shape):
+        return lax.broadcasted_iota(jnp.int32, shape, 1) < half
+
+    def pack(q, top, bottom):
+        if q == 0:
+            return jnp.where(side(top.shape), top, pltpu.roll(bottom, half, 1))
+        return jnp.where(side(top.shape), pltpu.roll(top, half, 1), bottom)
+
+    def unpack(q, packed):
+        turned = pltpu.roll(packed, half, 1)
+        return (packed, turned) if q == 0 else (turned, packed)
 
     def first_hop(s, i):
         away = span(i * wide + (1 - low) * h, h, 16)
         return remote(
-            r.part.at[s, away, :], r.got.at[s, strip(i), :], r.ex_s.at[s, 0, i], r.ex_r.at[s, 0, i], flip(0)
+            r.part.at[s, away, :], r.got.at[s, strip(i), :], r.ex_s.at[0], r.ex_r.at[s, 0, i], flip(0)
         )
 
     def wire_hop(s, bit, i):
         return remote(
             r.sent.at[s, bit - 1, strip(i), :],
             r.wire.at[s, bit - 1, strip(i), :],
-            r.ex_s.at[s, bit, i],
+            r.ex_s.at[bit],
             r.ex_r.at[s, bit, i],
             flip(bit),
         )
@@ -226,7 +242,7 @@
     def last_hop(s, i):
         at = own_part(i)
         return remote(
-            full[s].at[at, :], full[s].at[at, :], r.ex_s.at[s, bits, i], r.ex_r.at[s, bits, i], flip(0)
+            full[s].at[at, :], full[s].at[at, :], r.ex_s.at[bits], r.ex_r.at[s, bits, i], flip(0)
         )
 
     def pair_sum(s, i):
@@ -247,32 +263,42 @@
             full[s][own_part(i), :] = value
             last_hop(s, i).start()
 
-            @pl.when(i > 0)
+            @pl.when(i > begin)
             def _():
                 last_hop(s, i - 1).wait_recv()
-                use(chunk(i - 1))
-
+                use(i - 1, (1 - low) * h, h)
+
+            use(i, low * h, h)
             return 0
 
         lax.fori_loop(begin, end, step, 0)
-        if end == STEPS:
-            use(own_part(STEPS - 1))
-            last_hop(s, STEPS - 1).wait_recv()
-            use(span((STEPS - 1) * wide + (1 - low) * h, h, 16))
-
-    def linear_step(i, _):
-        value = contract_last(r.ups[i].reshape(2 * wide, width), tokens[...])
-        for s in range(2):
-            r.part[s, chunk(i), :] = value[s * wide : (s + 1) * wide].astype(BF)
-            first_hop(s, i).start()
-
-        @pl.when(i > 0)
-        def _():
-            pair_sum(0, i - 1)
-
+        last_hop(s, end - 1).wait_recv()
+        use(end - 1, (1 - low) * h, h)
+
+    def linear_step(p, _):
+        parts = []
+        for e in range(2):
+            i = 2 * p + e
+            value = contract_last(r.ups[i].reshape(2 * wide, width), tokens[...])
+            r.part[0, chunk(i), :] = value[:wide].astype(BF)
+            parts.append(value[wide:])
+            first_hop(0, i).start()
+            if e:
+                pair_sum(0, i - 1)
+            else:
+
+                @pl.when(p > 0)
+                def _():
+                    pair_sum(0, i - 1)
+
+        for q in (1, 0):
+            w = p + pairs * (1 - q)
+            r.part[1, chunk(w), :] = pack(q, *parts).astype(BF)
+            first_hop(1, w).start()
         return 0
 
-    def hidden_rows(at):
+    def hidden_rows(i, offset, size):
+        at = span(i * wide + offset, size, 16)
         activation, derivative, second_order = sigmoid_parts(r.full[0, at, :])
         hidden = activation.astype(BF)
         r.both[at, count:] = hidden
@@ -281,22 +307,44 @@
         r.acc[0] += contract_first(hidden, r.low_down[at, :])
         r.acc[1] += contract_first(hidden, r.outer_low[at, :])
 
-    def tangent_rows(at):
-        tangent = (r.derivative[at, :] * r.full[1, at, :].astype(F32)).astype(BF)
-        r.both[at, :count] = tangent
-        r.acc[1] += contract_first(tangent, r.low_down[at, :])
+    def unpacked(s, q, first, w, offset, size):
+        packed = full[s][span(w * wide + offset, size, 16), :].astype(F32)
+        p = w - first
+        return [
+            (span((2 * p + e) * wide + offset, size, 16), part)
+            for e, part in enumerate(unpack(q, packed))
+        ]
+
+    def both_rows(ref, ats):
+        return jnp.concatenate([ref[at, :] for at in ats], axis=0)
+
+    def tangent_rows(q):
+        at_q = lanes[q]
+
+        def use(w, offset, size):
+            ats, changes = [], []
+            for at, tangent in unpacked(1, q, pairs * (1 - q), w, offset, size):
+                change = (r.derivative[at, :] * tangent).astype(BF)
+                r.both[at, at_q] = change[:, at_q]
+                r.tangent[at, at_q] = tangent[:, at_q].astype(BF)
+                ats.append(at)
+                changes.append(change)
+            change = jnp.concatenate(changes, axis=0)
+            r.acc[1, at_q] += contract_first(change, both_rows(r.low_down, ats))[at_q]
+
+        return use
 
     def half_place(j):
         return span(across(j) * rows, rows, rows)
 
     def half_copy(s, j):
         return remote(
-            r.half_out.at[s, half_place(j), :], r.half_in.at[s, j], r.rx_s.at[s, j], r.rx_r.at[s, j], partner
+            r.half_out.at[s, half_place(j), :], r.half_in.at[s, j], r.rx_s.at[s], r.rx_r.at[s, j], partner
         )
 
     def column_copy(s, j):
         return remote(
-            r.column_out.at[s, j - 1], r.column_in.at[s, j - 1], r.rz_s.at[s, j - 1], r.rz_r.at[s, j - 1], column[j]
+            r.column_out.at[s, j - 1], r.column_in.at[s, j - 1], r.rz_s.at[s], r.rz_r.at[s], column[j]
         )
 
     def reduce_start(s):
@@ -315,16 +363,10 @@
 
     def reduce_end(s):
         value = pair_rows(s, 0)
+        drain(r.column_in.at[s], r.rz_r.at[s])
         for j in range(1, nz):
-            column_copy(s, j).wait_recv()
             value = value + r.column_in[s, j - 1].astype(F32)
         return value
-
-    def reduce_sent(s):
-        for j in range(nz):
-            half_copy(s, j).wait_send()
-            if j:
-                column_copy(s, j).wait_send()
 
     k_mine, k_other = span(low * half, half, half), span((1 - low) * half, half, half)
 
@@ -355,26 +397,27 @@
             gram_copy(j).start()
             return
         high = r.gram_full[...].astype(BF)
-        r.gram_parts[0] = high
-        r.gram_parts[1] = (r.gram_full[...] - high.astype(F32)).astype(BF)
-
-    lax.fori_loop(0, STEPS, linear_step, 0)
+        r.gram_parts[:, :count] = high
+        r.gram_parts[:, count:] = (r.gram_full[...] - high.astype(F32)).astype(BF)
+
+    lax.fori_loop(0, pairs, linear_step, 0)
     pair_sum(0, STEPS - 1)
     lax.fori_loop(0, STEPS, lambda i, _: (pair_sum(1, i), 0)[1], 0)
     gram_step(0)
     take_chunks(0, hidden_rows, 0, STEPS)
     reduce_start(0)
     gram_step(1)
-    take_chunks(1, tangent_rows, 0, STEPS - 1)
+    take_chunks(1, tangent_rows(1), 0, pairs)
+    reduce_start(1)
     reduce_middle(0)
-    take_chunks(1, tangent_rows, STEPS - 1, STEPS)
-    reduce_start(1)
+    take_chunks(1, tangent_rows(0), pairs, STEPS)
+    reduce_middle(1)
     for j in range(2, bits + 1):
         gram_step(j)
 
     same = jnp.where(own_row[0:1, :] == own_col, 1.0, 0.0)
-    for k, copy in enumerate(task_copies):
-        copy.wait_recv()
+    drain(r.task_slots, r.task_r)
+    for k in range(n - 1):
         same = same + jnp.where(r.task_slots[k, 0:1, :] == own_col, 1.0, 0.0)
     weight = 1.0 / (TASKS * jnp.sum(same, axis=1, keepdims=True))
 
@@ -382,7 +425,6 @@
     r.fresh[0] = (weight * (value - r.targets[...].astype(F32))).astype(BF)
     r.ee[block, :] = r.fresh[0]
     e_copies = spread(1, r.fresh.at[0], r.ee, 0)
-    reduce_middle(1)
 
     def gram_rows(i, _):
         at = chunk(i)
@@ -391,31 +433,7 @@
 
     r.both_gram[...] = jnp.zeros(r.both_gram.shape, F32)
     lax.fori_loop(0, STEPS, gram_rows, 0)
-    forward(1, r.ee, 0, e_copies)
-    value = reduce_end(1)
-    first = summed(weight * (value * value))
-    r.fresh[1] = (weight * value).astype(BF)
-    r.ee[span(count + zz * rows, rows, rows), :] = r.fresh[1]
-    t_copies = spread(2, r.fresh.at[1], r.ee, count)
-    arrived(e_copies)
-
-    def error_rows(i, kept):
-        at = chunk(i)
-        errors = r.ee[pl.ds(0, count), :]
-        back = contract_last(r.low_down[at, :], errors)
-        crossing = contract_last(r.outer_low[at, :], errors)
-        tangent = r.full[1, at, :].astype(F32)
-        curved = r.second[at, :] * back
-        r.curved[at, :] = curved
-        r.gate_base[at, :] = r.derivative[at, :] * crossing + curved * tangent
-        term = 2.0 * r.both[at, :count].astype(F32) * crossing + curved * tangent * tangent
-        return kept + folded(term)
-
-    kept = lax.fori_loop(0, STEPS, error_rows, jnp.zeros((8, count), F32))
-    first_part = summed(kept)
-    gram_step(bits + 1)
-
-    forward(2, r.ee, count, t_copies)
+
     def norm_rows(i, kept):
         for step in range(STEPS):
             one = r.ups[step, 1, span(i * 16, 16, 16), :].astype(F32)
@@ -424,49 +442,114 @@
         return kept
 
     norm = summed(lax.fori_loop(0, wide // 16, norm_rows, jnp.zeros((16, width), F32)))
-    arrived(t_copies)
-
-    def gate_step(i, _):
+    gram_step(bits + 1)
+    value = reduce_end(1)
+    first = summed(weight * (value * value))
+    r.fresh[1] = (weight * value).astype(BF)
+    r.ee[span(count + zz * rows, rows, rows), :] = r.fresh[1]
+    t_copies = spread(2, r.fresh.at[1], r.ee, count)
+    forward(1, r.ee, 0, e_copies)
+
+    own, over = lanes
+
+    def own_error_rows(i, _):
         at = chunk(i)
-        back = contract_last(r.low_down[at, :], r.ee[pl.ds(count, count), :])
-        r.part[2, at, :] = (r.gate_base[at, :] + r.derivative[at, :] * back).astype(BF)
-        first_hop(2, i).start()
-
-        @pl.when(i > 0)
-        def _():
-            pair_sum(2, i - 1)
-
+        errors = r.ee[pl.ds(0, half), :]
+        back = contract_last(r.low_down[at, :], errors)
+        crossing = contract_last(r.outer_low[at, :], errors)
+        curved = r.second[at, own] * back
+        r.curved[at, own] = curved
+        tangent = r.tangent[at, own].astype(F32)
+        r.gate_base[at, own] = r.derivative[at, own] * crossing + curved * tangent
         return 0
+
+    def over_error_rows(i, kept):
+        at = chunk(i)
+        crossing = contract_last(r.outer_low[at, :], r.ee[pl.ds(0, count), :])
+        tangent, curved = r.tangent[at, :].astype(F32), r.curved[at, :]
+        value = r.derivative[at, :] * crossing + curved * tangent
+        r.gate_base[at, over] = value[:, over]
+        term = 2.0 * r.both[at, :count].astype(F32) * crossing + curved * tangent * tangent
+        return kept + folded(term)
+
+    def gate_pair(q, p):
+        at = span(2 * p * wide, 2 * wide, 16)
+        w = p + pairs * q
+        if q == 0:
+            back = contract_last(r.low_down[at, :], r.ee[pl.ds(half, count), :])
+            back = pltpu.roll(back, half, 1)
+            r.curved[at, over] = r.second[at, over] * back[:, over]
+            value = r.gate_base[at, own] + r.derivative[at, own] * back[:, own]
+            packed = jnp.concatenate([value[:wide], value[wide:]], axis=1)
+        else:
+            back = contract_last(r.low_down[at, :], r.ee[pl.ds(count, count), :])
+            value = r.gate_base[at, :] + r.derivative[at, :] * back
+            packed = pack(1, value[:wide], value[wide:])
+        r.part[2, chunk(w), :] = packed.astype(BF)
+        first_hop(2, w).start()
+
+    def gate_side(q):
+        for p in range(pairs):
+            gate_pair(q, p)
+            if p:
+                pair_sum(2, pairs * q + p - 1)
+
+    def gate_rows(q):
+        at_q = lanes[q]
+
+        def use(w, offset, size):
+            ats = []
+            for at, part in unpacked(2, q, pairs * q, w, offset, size):
+                r.gate[at, at_q] = part[:, at_q].astype(BF)
+                ats.append(at)
+            if q == 0:
+                return
+            lowered = product(both_rows(r.gate, ats), r.gram_parts[...])
+            lowered = lowered[:, :count] + lowered[:, count:]
+            carried = (both_rows(r.derivative, ats) * lowered).astype(BF)
+            r.acc[2] += contract_first(carried, both_rows(r.low_down, ats))
+            for k, at in enumerate(ats):
+                r.carried[at, :] = carried[k * size : (k + 1) * size]
+            r.kept[...] += folded(both_rows(r.curved, ats) * lowered * lowered)
+
+        return use
 
     r.kept[...] = jnp.zeros(r.kept.shape, F32)
     r.gate_gram[...] = jnp.zeros(r.gate_gram.shape, F32)
     r.carry_gram[...] = jnp.zeros(r.carry_gram.shape, F32)
-
-    def gate_rows(at):
-        gate = r.gate[at, :]
-        lowered = product(gate, r.gram_parts[0]) + product(gate, r.gram_parts[1])
-        carried = (r.derivative[at, :] * lowered).astype(BF)
-        r.acc[2] += contract_first(carried, r.low_down[at, :])
-        r.gate_gram[...] += contract_first(gate, gate)
-        r.carry_gram[...] += contract_first(carried, r.both[at, :])
-        r.kept[...] += folded(r.curved[at, :] * lowered * lowered)
-
-    lax.fori_loop(0, STEPS, gate_step, 0)
-    pair_sum(2, STEPS - 1)
-    take_chunks(2, gate_rows, 0, STEPS)
+    lax.fori_loop(0, STEPS, own_error_rows, 0)
+    forward(2, r.ee, count, t_copies)
+    arrived(1)
+    gate_side(0)
+    kept = over_error_rows(0, jnp.zeros((8, count), F32))
+    pair_sum(2, pairs - 1)
+    kept = lax.fori_loop(1, STEPS, over_error_rows, kept)
+    arrived(2)
+    gate_side(1)
+    first_part = summed(kept)
     head, tail = pl.ds(0, count), pl.ds(count, count)
-    r.acc[2] += product(r.both_gram[tail, :].astype(BF), r.ee[...])
-    reduce_start(2)
-
+    r.acc[2] = product(r.both_gram[tail, :].astype(BF), r.ee[...])
     gram = contract_last(r.ee[...], r.ee[...])
     h_t = summed(r.both_gram[tail, head] * gram[count:, :count])
-    change = summed(r.gate_gram[...] * r.token_gram[...]) + 2.0 * h_t
-    change = change + summed(r.both_gram[head, head] * gram[:count, :count])
+    change = 2.0 * h_t + summed(r.both_gram[head, head] * gram[:count, :count])
     change = change + summed(r.both_gram[tail, tail] * gram[count:, count:])
-    carry = summed(r.carry_gram[:, head] * gram[:count, :count])
-    carry = carry + summed(r.carry_gram[:, tail] * gram[:count, count:])
+    r.error_gram[...] = gram[:count, :]
+    pair_sum(2, STEPS - 1)
+    take_chunks(2, gate_rows(0), 0, pairs)
+    take_chunks(2, gate_rows(1), pairs, STEPS)
+    reduce_start(2)
+
+    def late_rows(i, _):
+        at = chunk(i)
+        gate = r.gate[at, :]
+        r.gate_gram[...] += contract_first(gate, gate)
+        r.carry_gram[...] += contract_first(r.carried[at, :], r.both[at, :])
+        return 0
+
+    lax.fori_loop(0, STEPS, late_rows, 0)
+    change = change + summed(r.gate_gram[...] * r.token_gram[...])
+    carry = summed(r.carry_gram[...] * r.error_gram[...])
     final = summed(r.kept[...]) + 2.0 * carry
-
     reduce_middle(2)
     value = reduce_end(2)
     final = final + summed(weight * (value * value))
@@ -476,13 +559,13 @@
         value = value + jnp.where(index == at, number, 0.0)
     r.own[...] = value
     number_copies = [
-        remote(r.own, r.slots.at[k], r.all_s.at[k], r.all_r.at[k], all_places[k])
+        remote(r.own, r.slots.at[k], r.all_s, r.all_r, all_places[k])
         for k in range(n * m - 1)
     ]
     for copy in number_copies:
         copy.start()
-    for k, copy in enumerate(number_copies):
-        copy.wait_recv()
+    drain(r.slots, r.all_r)
+    for k in range(n * m - 1):
         value = value + r.slots[k]
     norm, first, change, final = (summed(jnp.where(index == at, value, 0.0)) for at in range(4))
     step = norm / (norm + first)
@@ -500,21 +583,15 @@
     r.sums[0:1, :] = jnp.broadcast_to(step + step_next * (ratio + keep), (1, 128))
     r.sums[1:2, :] = jnp.broadcast_to(-step_next * step, (1, 128))
 
-    def sends_done(i, _):
-        for s in range(3):
-            first_hop(s, i).wait_send()
-            for bit in range(1, bits):
-                wire_hop(s, bit, i).wait_send()
-            last_hop(s, i).wait_send()
-        return 0
-
-    lax.fori_loop(0, STEPS, sends_done, 0)
-    for j in range(bits + 1):
-        gram_copy(j).wait_send()
-    for copy in token_copies + e_copies + t_copies + task_copies + number_copies:
-        copy.wait_send()
-    for s in range(3):
-        reduce_sent(s)
+    for hop in range(bits + 1):
+        drain(r.got, r.ex_s.at[hop])
+        gram_copy(hop).wait_send()
+    for k in range(3):
+        drain(r.xx.at[pl.ds(0, (n - 1) * rows), :], r.sp_s.at[k])
+        drain(r.half_out.at[k], r.rx_s.at[k])
+        drain(r.column_out.at[k], r.rz_s.at[k])
+    drain(r.task_slots, r.task_s)
+    drain(r.slots, r.all_s)
 
 
 def fused(n, m, tokens, targets, task, up, outer_up, down, outer_down):
@@ -541,7 +618,8 @@
         "got": vm((3, hp, count), BF),
         "sent": vm((3, links, hp, count), BF),
         "wire": vm((3, links, hp, count), BF),
-        "full": vm((2, total, count), BF),
+        "full": vm((3, total, count), BF),
+        "tangent": vm((total, count), BF),
         "derivative": vm((total, count), F32),
         "second": vm((total, count), F32),
         "curved": vm((total, count), F32),
@@ -557,10 +635,12 @@
         "gram_sent": vm((links, half, count), F32),
         "gram_wire": vm((links, half, count), F32),
         "gram_full": vm((count, count), F32),
-        "gram_parts": vm((2, count, count), BF),
+        "gram_parts": vm((count, 2 * count), BF),
         "both_gram": vm((2 * count, 2 * count), F32),
         "gate_gram": vm((count, count), F32),
         "carry_gram": vm((count, 2 * count), F32),
+        "error_gram": vm((count, 2 * count), F32),
+        "carried": vm((total, count), BF),
         "kept": vm((8, count), F32),
         "tokens": vm(tokens.shape, BF),
         "targets": vm(targets.shape, BF),
@@ -570,23 +650,22 @@
         "own": vm((1, 128), F32),
         "slots": vm((n * m - 1, 1, 128), F32),
         "small_sem": dma((3,)),
-        "load_sem": dma((4, STEPS)),
-        "task_s": dma((n - 1,)),
-        "task_r": dma((n - 1,)),
-        "sp_zs": dma((3, nz - 1)),
+        "load_sem": dma((4,)),
+        "task_s": dma,
+        "task_r": dma,
+        "sp_s": dma((3,)),
         "sp_zr": dma((3, nz - 1)),
-        "sp_xs": dma((3, nz)),
-        "sp_xr": dma((3, nz)),
-        "ex_s": dma((3, bits + 1, STEPS)),
+        "sp_xr": dma((3,)),
+        "ex_s": dma((bits + 1,)),
         "ex_r": dma((3, bits + 1, STEPS)),
-        "rx_s": dma((3, nz)),
+        "rx_s": dma((3,)),
         "rx_r": dma((3, nz)),
-        "rz_s": dma((3, nz - 1)),
-        "rz_r": dma((3, nz - 1)),
+        "rz_s": dma((3,)),
+        "rz_r": dma((3,)),
         "gram_s": dma((bits + 1,)),
         "gram_r": dma((bits + 1,)),
-        "all_s": dma((n * m - 1,)),
-        "all_r": dma((n * m - 1,)),
+        "all_s": dma,
+        "all_r": dma,
     }
     inputs = ("task_in", "tokens_in", "targets_in", "up", "outer_up", "down", "outer_down")
     arrays = (task, tokens, targets, up, outer_up, down, outer_down)
@@ -619,25 +698,20 @@
     hid, width = meta_up.shape
     of_outer, of_change = sums[0:1, 0:1], sums[1:2, 0:1]
     wide = ups.shape[2]
-    copies = []
-    for i, (start, size) in enumerate(output_tiles(hid, wide)):
+    for start, size in output_tiles(hid, wide):
         at, part = pl.ds(start, size), pl.ds(start % wide, size)
         outer = ups[start // wide, 1, part, :].astype(F32)
         stage[0, at, :] = of_outer * outer + of_change * product(gate[at, :], xx[...])
         outer = outer_low[at, :].astype(F32)
         stage[1, at, :] = of_outer * outer + of_change * product(both[at, :], ee[...])
         for k, meta in enumerate((meta_up, meta_down)):
-            copies.append(
-                pltpu.make_async_copy(stage.at[k, at, :], meta.at[at, :], sems.at[k, i])
-            )
-            copies[-1].start()
-    for copy in copies:
-        copy.wait()
+            pltpu.make_async_copy(stage.at[k, at, :], meta.at[at, :], sems.at[k]).start()
+    for k, meta in enumerate((meta_up, meta_down)):
+        pltpu.make_async_copy(stage.at[k], meta, sems.at[k]).wait()
 
 
 def outputs(hid, gate, both, xx, ee, ups, outer_low, sums):
     width = xx.shape[1]
-    tiles = len(output_tiles(hid, ups.shape[2]))
     return pl.pallas_call(
         output_kernel,
         out_shape=[jax.ShapeDtypeStruct((hid, width), F32)] * 2,
@@ -645,7 +719,7 @@
         out_specs=[pl.BlockSpec(memory_space=pltpu.HBM)] * 2,
         scratch_shapes=[
             pltpu.VMEM((2, hid, width), F32),
-            pltpu.SemaphoreType.DMA((2, tiles)),
+            pltpu.SemaphoreType.DMA((2,)),
         ],
         compiler_params=pltpu.CompilerParams(vmem_limit_bytes=OUT_LIMIT),
     )(gate, both, xx, ee, ups, outer_low, sums)

time: 82.8 us -> 79.5 us (0.960)
  Pallas kernels: 82 us -> 78.5 us
    pallas_call x1, Pallas kernels: 75.5 us -> 72.2 us  [fused(): pl.pallas_call(functools.partial(fused_kernel, n, m, hid, inputs + tuple(...]
where the time goes in v3:
time: 79.5 us; the launch traced here: 79.3 us
  Pallas kernels  78.5 us (99%)
  between operations  0.8 us (1%)
    pallas_call x1, Pallas kernels, fused(): pl.pallas_call(functools.partial(fused_kernel, n, m, hid, inputs + tuple(...  72.2 us
    pallas_call x1, Pallas kernels, outputs(): pl.pallas_call(output_kernel, out_shape=[jax.ShapeDtypeStruct((hid, width...  6.36 us

profile of v3, /device:TPU:0, one launch (start us, length us, event | category | flops | bytes accessed | tf_op | source)
XLA Modules:
  0.0 79.3 jit_solution(6412445351448038929)
XLA Ops:
  0.6 72.2 %shard_map.86 = (bf16[2432,128]{1,0:T(8,128)(2,1)S(1)}, bf16[2432,256]{1,0:T(8,128)(2,1)S(1)}, bf16[128,896]{1,0:T(8,128)(2,1)S(1)}, bf16[256,896]{1,0:T(8,128)(...) custom-call(s32[16]{0:T(128)} %refs_0_.1, ...), custom_call_target="tpu_custom_call" | custom-call | tf_op jit(solution)/shard_map/pallas_call | solution.py:673
  72.8 6.4 %shard_map.87 = (f32[2368,896]{1,0:T(8,128)}, f32[2368,896]{1,0:T(8,128)}) custom-call(bf16[2432,128]{1,0:T(8,128)(2,1)S(1)} %get-tuple-element.9.gate, bf16[2432,256]{1,0:T(8,128)(2,1)S(1)} %get-tuple-element.10.both, bf16[128,896]{1,0:T(8,128)(2,1)S(1)} %get-tuple-element.11.xx, bf16[256,896]{1,0:T(8,128)(2,1)S(1)} %get-tuple-element.12.ee, ...), custom_call_target="tpu_custom_call" | custom-call | tf_op jit(solution)/shard_map/pallas_call | solution.py:715

commit v4 on v3

--- a/solution.py
+++ b/solution.py
@@ -251,7 +251,7 @@
         r.sent[s, 0, strip(i), :] = value.astype(BF)
         wire_hop(s, 1, i).start()
 
-    def take_chunks(s, use, begin, end):
+    def take_chunks(s, use, begin, end, prompt=False):
         def step(i, _):
             for bit in range(1, bits):
                 wire_hop(s, bit, i).wait_recv()
@@ -262,6 +262,11 @@
                     wire_hop(s, bit + 1, i).start()
             full[s][own_part(i), :] = value
             last_hop(s, i).start()
+            if prompt:
+                use(i, low * h, h)
+                last_hop(s, i).wait_recv()
+                use(i, (1 - low) * h, h)
+                return 0
 
             @pl.when(i > begin)
             def _():
@@ -272,8 +277,9 @@
             return 0
 
         lax.fori_loop(begin, end, step, 0)
-        last_hop(s, end - 1).wait_recv()
-        use(end - 1, (1 - low) * h, h)
+        if not prompt:
+            last_hop(s, end - 1).wait_recv()
+            use(end - 1, (1 - low) * h, h)
 
     def linear_step(p, _):
         parts = []
@@ -488,12 +494,6 @@
         r.part[2, chunk(w), :] = packed.astype(BF)
         first_hop(2, w).start()
 
-    def gate_side(q):
-        for p in range(pairs):
-            gate_pair(q, p)
-            if p:
-                pair_sum(2, pairs * q + p - 1)
-
     def gate_rows(q):
         at_q = lanes[q]
 
@@ -520,12 +520,18 @@
     lax.fori_loop(0, STEPS, own_error_rows, 0)
     forward(2, r.ee, count, t_copies)
     arrived(1)
-    gate_side(0)
-    kept = over_error_rows(0, jnp.zeros((8, count), F32))
-    pair_sum(2, pairs - 1)
-    kept = lax.fori_loop(1, STEPS, over_error_rows, kept)
-    arrived(2)
-    gate_side(1)
+    for p in range(pairs):
+        gate_pair(0, p)
+        if p:
+            pair_sum(2, p - 1)
+    kept = jnp.zeros((8, count), F32)
+    for p in range(pairs):
+        kept = over_error_rows(2 * p, kept)
+        pair_sum(2, pairs + p - 1)
+        kept = over_error_rows(2 * p + 1, kept)
+        if p == 0:
+            arrived(2)
+        gate_pair(1, p)
     first_part = summed(kept)
     head, tail = pl.ds(0, count), pl.ds(count, count)
     r.acc[2] = product(r.both_gram[tail, :].astype(BF), r.ee[...])
@@ -536,7 +542,7 @@
     r.error_gram[...] = gram[:count, :]
     pair_sum(2, STEPS - 1)
     take_chunks(2, gate_rows(0), 0, pairs)
-    take_chunks(2, gate_rows(1), pairs, STEPS)
+    take_chunks(2, gate_rows(1), pairs, STEPS, prompt=True)
     reduce_start(2)
 
     def late_rows(i, _):
@@ -551,6 +557,7 @@
     carry = summed(r.carry_gram[...] * r.error_gram[...])
     final = summed(r.kept[...]) + 2.0 * carry
     reduce_middle(2)
+
     value = reduce_end(2)
     final = final + summed(weight * (value * value))
     index = lax.broadcasted_iota(jnp.int32, (1, 128), 1)

time: 79.5 us -> 79.1 us (level)
  no operation moved by 1% of the time
where the time goes in v4:
time: 79.1 us; the launch traced here: 78.9 us
  Pallas kernels  78.1 us (99%)
  between operations  0.8 us (1%)
    pallas_call x1, Pallas kernels, fused(): pl.pallas_call(functools.partial(fused_kernel, n, m, hid, inputs + tuple(...  71.7 us
    pallas_call x1, Pallas kernels, outputs(): pl.pallas_call(output_kernel, out_shape=[jax.ShapeDtypeStruct((hid, width...  6.35 us

profile of v4, /device:TPU:0, one launch (start us, length us, event | category | flops | bytes accessed | tf_op | source)
XLA Modules:
  0.0 78.9 jit_solution(8042805754532869063)
XLA Ops:
  0.6 71.7 %shard_map.86 = (bf16[2432,128]{1,0:T(8,128)(2,1)S(1)}, bf16[2432,256]{1,0:T(8,128)(2,1)S(1)}, bf16[128,896]{1,0:T(8,128)(2,1)S(1)}, bf16[256,896]{1,0:T(8,128)(...) custom-call(s32[16]{0:T(128)} %refs_0_.1, ...), custom_call_target="tpu_custom_call" | custom-call | tf_op jit(solution)/shard_map/pallas_call | solution.py:680
  72.4 6.4 %shard_map.87 = (f32[2368,896]{1,0:T(8,128)}, f32[2368,896]{1,0:T(8,128)}) custom-call(bf16[2432,128]{1,0:T(8,128)(2,1)S(1)} %get-tuple-element.9.gate, bf16[2432,256]{1,0:T(8,128)(2,1)S(1)} %get-tuple-element.10.both, bf16[128,896]{1,0:T(8,128)(2,1)S(1)} %get-tuple-element.11.xx, bf16[256,896]{1,0:T(8,128)(2,1)S(1)} %get-tuple-element.12.ee, ...), custom_call_target="tpu_custom_call" | custom-call | tf_op jit(solution)/shard_map/pallas_call | solution.py:722

commit v5 on v4

--- a/solution.py
+++ b/solution.py
@@ -440,14 +440,19 @@
     r.both_gram[...] = jnp.zeros(r.both_gram.shape, F32)
     lax.fori_loop(0, STEPS, gram_rows, 0)
 
-    def norm_rows(i, kept):
+    def low_squares(i, kept):
+        for step in range(STEPS):
+            one = r.outer_low[span(step * wide + i * 16, 16, 16), :].astype(F32)
+            kept = kept + one * one
+        return kept
+
+    def up_squares(i, kept):
         for step in range(STEPS):
             one = r.ups[step, 1, span(i * 16, 16, 16), :].astype(F32)
-            two = r.outer_low[span(step * wide + i * 16, 16, 16), :].astype(F32)
-            kept = kept + one * one + two * two
+            kept = kept + one * one
         return kept
 
-    norm = summed(lax.fori_loop(0, wide // 16, norm_rows, jnp.zeros((16, width), F32)))
+    norm = summed(lax.fori_loop(0, wide // 16, low_squares, jnp.zeros((16, width), F32)))
     gram_step(bits + 1)
     value = reduce_end(1)
     first = summed(weight * (value * value))
@@ -557,6 +562,7 @@
     carry = summed(r.carry_gram[...] * r.error_gram[...])
     final = summed(r.kept[...]) + 2.0 * carry
     reduce_middle(2)
+    norm = norm + summed(lax.fori_loop(0, wide // 16, up_squares, jnp.zeros((16, width), F32)))
 
     value = reduce_end(2)
     final = final + summed(weight * (value * value))

time: 79.1 us -> 79.1 us (level)
  no operation moved by 1% of the time
where the time goes in v5:
time: 79.1 us; the launch traced here: 78.9 us
  Pallas kernels  78.1 us (99%)
  between operations  0.8 us (1%)
    pallas_call x1, Pallas kernels, fused(): pl.pallas_call(functools.partial(fused_kernel, n, m, hid, inputs + tuple(...  71.7 us
    pallas_call x1, Pallas kernels, outputs(): pl.pallas_call(output_kernel, out_shape=[jax.ShapeDtypeStruct((hid, width...  6.36 us

profile of v5, /device:TPU:0, one launch (start us, length us, event | category | flops | bytes accessed | tf_op | source)
XLA Modules:
  0.0 78.9 jit_solution(2351744197385445933)
XLA Ops:
  0.6 71.7 %shard_map.86 = (bf16[2432,128]{1,0:T(8,128)(2,1)S(1)}, bf16[2432,256]{1,0:T(8,128)(2,1)S(1)}, bf16[128,896]{1,0:T(8,128)(2,1)S(1)}, bf16[256,896]{1,0:T(8,128)(...) custom-call(s32[16]{0:T(128)} %refs_0_.1, ...), custom_call_target="tpu_custom_call" | custom-call | tf_op jit(solution)/shard_map/pallas_call | solution.py:686
  72.4 6.4 %shard_map.87 = (f32[2368,896]{1,0:T(8,128)}, f32[2368,896]{1,0:T(8,128)}) custom-call(bf16[2432,128]{1,0:T(8,128)(2,1)S(1)} %get-tuple-element.9.gate, bf16[2432,256]{1,0:T(8,128)(2,1)S(1)} %get-tuple-element.10.both, bf16[128,896]{1,0:T(8,128)(2,1)S(1)} %get-tuple-element.11.xx, bf16[256,896]{1,0:T(8,128)(2,1)S(1)} %get-tuple-element.12.ee, ...), custom_call_target="tpu_custom_call" | custom-call | tf_op jit(solution)/shard_map/pallas_call | solution.py:728
